TPU v7x, 32 devices: a whole 2x2x4 slice. The times are simulated.
32 devices in a mesh: groups: 2 (over y), seq: 4 (over z), head: 2 (over x), sub: 2 (over core).
Axes of the slice: x: 2, y: 2, z: 4, core: 2. Of those that a mesh axis runs over, the one named last changes fastest.
Arguments:
- queries: bfloat16 [32, 64, 8192], P(('groups', 'seq'), None, 'head'), parts along dimension 0, may hold values from -6 to 6
- new_kv: bfloat16 [32, 64, 2, 1024], P(('groups', 'seq'), None, None, 'head'), parts along dimension 0, may hold values from -6 to 6
- kv_pages: bfloat16 [336, 2, 128, 1024], P(('groups', 'seq', 'sub'), None, None, 'head'), parts along dimension 0, may hold values from -6 to 6
- page_table: int32 [32, 16], P('groups'), parts along dimension 0, may hold values from -1 to 167, as said below
- cached_len: int32 [32], P('groups'), parts along dimension 0, may hold values from 1 to 2048, as said below
- is_prefill: int32 [32], P('groups'), parts along dimension 0, may hold values from 0 to 1, as said below
Outputs:
- attended: bfloat16 [32, 64, 8192], P(('groups', 'seq'), None, 'head'), parts along dimension 0
There are 2 independent parts, one for each index of `groups`. A program takes and returns all parts, laid end to end along the dimension named above; each array names one. Nothing has to cross between parts.
Inputs may be any that keep to these rules, and one draw needn't show every extreme that they name: `page_table`: entry [s, p] is the page number of page p of sequence s for p < ceil(cached_len[s] / 128) and -1 after; page number q lies on owner q // 21 (owner index = seq index * 2 + sub index) in its slot q % 21. Listing the pages of all sequences in order of sequence and page as t = 0, 1, ..., page t has owner (t + c) % 8 and slot (t + c) // 8 for one drawn c. No owner holds more than 8 page of the 4 sequences of one seq shard, and some owner holds exactly 8. `cached_len`: A decode sequence has 1 to 4 cache pages, a prefill sequence 8 to 16; all 4 sequences of one drawn seq shard are prefill sequences with 16 pages. `is_prefill`: exactly 8 sequences are prefill sequences.
All inputs are finite; a program needn't handle non-finite values.
Results may differ from a plain program's by a relative error of at most 0.014.
Values may be sent and summed in bfloat16 or wider, within the bound.
A program may use at most 64 MiB of HBM per device.

v0:
```python
import functools

import jax
import jax.numpy as jnp
from jax import lax
from jax.experimental import pallas as pl
from jax.experimental.pallas import tpu as pltpu
from jax.sharding import PartitionSpec as P

HD = 128
PAGE = 128


NEG_FILL = -1e30


def partial_softmax(
    query_heads, cache_keys, cache_values, cache_valid, fresh_keys, fresh_values, fresh_valid
):
    score_scale = HD ** (-0.5)
    cache_scores = (
        jnp.einsum("rkgd,nkd->kgrn", query_heads, cache_keys, preferred_element_type=jnp.float32)
        * score_scale
    )
    fresh_scores = (
        jnp.einsum("rkgd,jkd->kgrj", query_heads, fresh_keys, preferred_element_type=jnp.float32)
        * score_scale
    )
    cache_mask = cache_valid[None, None, None, :]
    fresh_mask = fresh_valid[None, None, :, :]
    peak = jnp.maximum(
        jnp.max(jnp.where(cache_mask, cache_scores, NEG_FILL), axis=-1),
        jnp.max(jnp.where(fresh_mask, fresh_scores, NEG_FILL), axis=-1),
    )
    cache_weights = jnp.where(cache_mask, jnp.exp(cache_scores - peak[..., None]), 0.0)
    fresh_weights = jnp.where(fresh_mask, jnp.exp(fresh_scores - peak[..., None]), 0.0)
    weight_sum = jnp.sum(cache_weights, axis=-1) + jnp.sum(fresh_weights, axis=-1)
    numerator = jnp.einsum(
        "kgrn,nkd->kgrd",
        cache_weights.astype(jnp.bfloat16),
        cache_values,
        preferred_element_type=jnp.float32,
    )
    numerator = numerator + jnp.einsum(
        "kgrj,jkd->kgrd",
        fresh_weights.astype(jnp.bfloat16),
        fresh_values,
        preferred_element_type=jnp.float32,
    )
    return (peak, weight_sum, numerator)


def attend_all(
    query_block, fresh_block, received, fetch_index, page_here, lengths, live_rows, causal, fresh_on
):
    kv_width = received.shape[-1]
    heads_kv = kv_width // HD
    row_count = query_block.shape[1]
    group_size = query_block.shape[2] // kv_width
    page_count = fetch_index.shape[1]
    positions = jnp.arange(page_count * PAGE, dtype=jnp.int32)

    def one_sequence(inputs):
        query_rows, fresh_rows, index_row, here_row, length, live_row = inputs
        fetched = jnp.take(received, index_row, axis=0)
        cache_keys = fetched[:, 0].reshape(page_count * PAGE, heads_kv, HD)
        cache_values = fetched[:, 1].reshape(page_count * PAGE, heads_kv, HD)
        page_mask = jnp.broadcast_to(here_row[:, None], (page_count, PAGE)).reshape(
            page_count * PAGE
        )
        cache_valid = page_mask & (positions < length)
        query_heads = query_rows.reshape(row_count, heads_kv, group_size, HD)
        fresh_keys = fresh_rows[:, 0].reshape(row_count, heads_kv, HD)
        fresh_values = fresh_rows[:, 1].reshape(row_count, heads_kv, HD)
        fresh_valid = causal & live_row[:, None] & fresh_on
        return partial_softmax(
            query_heads,
            cache_keys,
            cache_values,
            cache_valid,
            fresh_keys,
            fresh_values,
            fresh_valid,
        )

    return lax.map(
        one_sequence, (query_block, fresh_block, fetch_index, page_here, lengths, live_rows)
    )


def finish(weight_sum, numerator, live_rows):
    unused_rows = 1.0 - live_rows.astype(jnp.float32)
    attended = numerator / (weight_sum + unused_rows[:, None, None, :])[..., None]
    attended = jnp.where(live_rows[:, None, None, :, None], attended, 0.0)
    seq_dev, heads_kv, group_size, row_count, head_dim = attended.shape
    return (
        jnp.transpose(attended, (0, 3, 1, 2, 4))
        .reshape(seq_dev, row_count, heads_kv * group_size * head_dim)
        .astype(jnp.bfloat16)
    )


def exchange_pages(queries, new_kv, kv_pages, page_table, cached_len, is_prefill):
    seq_shards = lax.axis_size("seq")
    sub_count = lax.axis_size("sub")
    owners = seq_shards * sub_count
    seq_index = lax.axis_index("seq")
    core_index = lax.axis_index("sub")
    owner_self = seq_index * sub_count + core_index
    seq_dev, row_count, query_width = queries.shape
    pages_dev = kv_pages.shape[0]
    kv_width = kv_pages.shape[3]
    page_count = page_table.shape[1]
    entries = seq_dev * page_count
    capacity = (entries + owners - 1) // owners
    table_rows = page_table.reshape(seq_shards, entries)
    holder = jnp.where(table_rows >= 0, table_rows // pages_dev, -1)
    slot_of = jnp.where(table_rows >= 0, table_rows % pages_dev, 0)
    owned_here = holder == owner_self
    rank_among = jnp.cumsum(owned_here.astype(jnp.int32), axis=1) - 1
    picked = owned_here[:, :, None] & (
        rank_among[:, :, None] == jnp.arange(capacity, dtype=jnp.int32)[None, None, :]
    )
    send_slots = jnp.sum(jnp.where(picked, slot_of[:, :, None], 0), axis=1).reshape(
        seq_shards * capacity
    )
    first_seq = seq_index * seq_dev
    my_table = lax.dynamic_slice_in_dim(page_table, first_seq, seq_dev, 0)
    my_lengths = lax.dynamic_slice_in_dim(cached_len, first_seq, seq_dev, 0)
    my_flags = lax.dynamic_slice_in_dim(is_prefill, first_seq, seq_dev, 0)
    flat_table = my_table.reshape(entries)
    my_holder = jnp.where(flat_table >= 0, flat_table // pages_dev, -1)
    entry_order = jnp.arange(entries, dtype=jnp.int32)
    earlier = (my_holder[:, None] == my_holder[None, :]) & (
        entry_order[None, :] < entry_order[:, None]
    )
    my_rank = jnp.sum(earlier.astype(jnp.int32), axis=1)
    row_ids = jnp.arange(row_count, dtype=jnp.int32)
    live_rows = (my_flags[:, None] == 1) | (row_ids[None, :] == 0)
    causal = row_ids[None, :] <= row_ids[:, None]
    part_width = kv_width // sub_count
    split_pages = kv_pages.reshape(pages_dev, 2, PAGE, sub_count, part_width)
    chosen = jnp.take(split_pages, send_slots, axis=0).reshape(
        seq_shards, capacity, 2, PAGE, sub_count, part_width
    )
    outgoing = jnp.moveaxis(chosen, 4, 1).reshape(owners, capacity, 2, PAGE, part_width)
    received = lax.all_to_all(
        outgoing, ("seq", "sub"), split_axis=0, concat_axis=0, tiled=True
    ).reshape(owners * capacity, 2, PAGE, part_width)
    present = flat_table >= 0
    fetch_index = jnp.where(present, my_holder * capacity + my_rank, 0)
    query_part = query_width // sub_count
    my_queries = lax.dynamic_slice_in_dim(queries, core_index * query_part, query_part, 2)
    my_fresh = lax.dynamic_slice_in_dim(new_kv, core_index * part_width, part_width, 3)
    peak, weight_sum, numerator = attend_all(
        my_queries,
        my_fresh,
        received,
        fetch_index.reshape(seq_dev, page_count),
        present.reshape(seq_dev, page_count),
        my_lengths,
        live_rows,
        causal,
        core_index >= 0,
    )
    own_heads = finish(weight_sum, numerator, live_rows)
    return lax.all_gather(own_heads, "sub", axis=2, tiled=True)


MESH = pl.DeviceIdType.MESH
SCALE = HD ** (-0.5)
LOG2E = 1.4426950408889634


def greet(z, n):
    has_left, has_right = z > 0, z < n - 1
    barrier = pltpu.get_barrier_semaphore()

    @pl.when(has_left)
    def _():
        pl.semaphore_signal(barrier, inc=1, device_id={"seq": z - 1}, device_id_type=MESH)

    @pl.when(has_right)
    def _():
        pl.semaphore_signal(barrier, inc=1, device_id={"seq": z + 1}, device_id_type=MESH)

    pl.semaphore_wait(barrier, has_left.astype(jnp.int32) + has_right.astype(jnp.int32))
    return has_left, has_right


def remote(src, dst, send, recv, z):
    return pltpu.make_async_remote_copy(
        src_ref=src, dst_ref=dst, send_sem=send, recv_sem=recv,
        device_id={"seq": z}, device_id_type=MESH,
    )


DEC_MAXP = 4


def line_steps(z, n, count, lag, from_left, from_right, last):
    def guarded(c, work):
        @pl.when((c >= 0) & (c < count))
        def _():
            work(c)

    def step(s, carry):
        guarded(s - lag * z, from_left)
        guarded(s - lag * (n - 1 - z), from_right)
        guarded(s - lag * jnp.maximum(z, n - 1 - z), last)
        return carry

    lax.fori_loop(0, count + lag * (n - 1), step, 0)


def gather_queries_kernel(n, count, own, out, rin, rout, lin, lout, rs, rr, ls, lr):
    z = lax.axis_index("seq")
    has_left, has_right = greet(z, n)

    def right(c):
        return remote(rout.at[c], rin.at[c], rs.at[c], rr.at[c], z + 1)

    def left(c):
        return remote(lout.at[c], lin.at[c], ls.at[c], lr.at[c], z - 1)

    def from_left(c):
        @pl.when(has_left)
        def _():
            right(c).wait_recv()
            rout[c] = own[c] + rin[c]

        @pl.when(jnp.logical_not(has_left))
        def _():
            rout[c] = own[c]

        @pl.when(has_right)
        def _():
            right(c).start()

    def from_right(c):
        @pl.when(has_right)
        def _():
            left(c).wait_recv()
            lout[c] = own[c] + lin[c]

        @pl.when(jnp.logical_not(has_right))
        def _():
            lout[c] = own[c]

        @pl.when(has_left)
        def _():
            left(c).start()

    def last(c):
        @pl.when(has_right)
        def _():
            out[c] = rout[c] + lin[c]

        @pl.when(jnp.logical_not(has_right))
        def _():
            out[c] = rout[c]

    line_steps(z, n, count, 4, from_left, from_right, last)

    def drain(c, carry):
        @pl.when(has_right)
        def _():
            right(c).wait_send()

        @pl.when(has_left)
        def _():
            left(c).wait_send()

        return carry

    lax.fori_loop(0, count, drain, 0)


def gather_queries(own, n):
    total, width = own.shape
    rows = 16
    count = total // rows
    shape = (count, rows, width)
    buffer = pltpu.VMEM(shape, own.dtype)
    return pl.pallas_call(
        functools.partial(gather_queries_kernel, n, count),
        out_shape=jax.ShapeDtypeStruct(shape, own.dtype),
        in_specs=[pl.BlockSpec(memory_space=pltpu.VMEM)],
        out_specs=pl.BlockSpec(memory_space=pltpu.VMEM),
        scratch_shapes=[buffer] * 4 + [pltpu.SemaphoreType.DMA((count,))] * 4,
        compiler_params=pltpu.CompilerParams(collective_id=0, has_side_effects=True),
        name="gather_queries",
    )(own.reshape(shape)).reshape(total, width)


def merge(o1, e1, o2, e2):
    top = jnp.maximum(e1, e2)
    w1, w2 = jnp.exp(e1 - top), jnp.exp(e2 - top)
    total = w1 + w2
    inv = 1.0 / total
    return o1 * (w1 * inv) + o2 * (w2 * inv), top + jnp.log(total)


def reduce_outputs_kernel(
    n, count, o, e, out, oute, ri, ro, li, lo, rei, reo, lei, leo, rs, rr, ls, lr, res, rer, les, ler
):
    z = lax.axis_index("seq")
    has_left, has_right = greet(z, n)

    def right(c):
        return (
            remote(ro.at[c], ri.at[c], rs.at[c], rr.at[c], z + 1),
            remote(reo.at[c], rei.at[c], res.at[c], rer.at[c], z + 1),
        )

    def left(c):
        return (
            remote(lo.at[c], li.at[c], ls.at[c], lr.at[c], z - 1),
            remote(leo.at[c], lei.at[c], les.at[c], ler.at[c], z - 1),
        )

    def join(o1, e1, o2, e2, oo, eo, c):
        joined, stat = merge(o1[c].astype(jnp.float32), e1[c], o2[c].astype(jnp.float32), e2[c])
        oo[c] = joined.astype(oo.dtype)
        eo[c] = stat

    def from_left(c):
        @pl.when(has_left)
        def _():
            for x in right(c):
                x.wait_recv()
            join(o, e, ri, rei, ro, reo, c)

        @pl.when(jnp.logical_not(has_left))
        def _():
            ro[c] = o[c]
            reo[c] = e[c]

        @pl.when(has_right)
        def _():
            for x in right(c):
                x.start()

    def from_right(c):
        @pl.when(has_right)
        def _():
            for x in left(c):
                x.wait_recv()
            join(o, e, li, lei, lo, leo, c)

        @pl.when(jnp.logical_not(has_right))
        def _():
            lo[c] = o[c]
            leo[c] = e[c]

        @pl.when(has_left)
        def _():
            for x in left(c):
                x.start()

    def last(c):
        @pl.when(has_right)
        def _():
            join(ro, reo, li, lei, out, oute, c)

        @pl.when(jnp.logical_not(has_right))
        def _():
            out[c] = ro[c]
            oute[c] = reo[c]

    line_steps(z, n, count, 2, from_left, from_right, last)

    def drain(c, carry):
        @pl.when(has_right)
        def _():
            for x in right(c):
                x.wait_send()

        @pl.when(has_left)
        def _():
            for x in left(c):
                x.wait_send()

        return carry

    lax.fori_loop(0, count, drain, 0)


def reduce_outputs(o, e, n):
    count = e.shape[0]
    return pl.pallas_call(
        functools.partial(reduce_outputs_kernel, n, count),
        out_shape=[jax.ShapeDtypeStruct(x.shape, x.dtype) for x in (o, e)],
        in_specs=[pl.BlockSpec(memory_space=pltpu.VMEM)] * 2,
        out_specs=[pl.BlockSpec(memory_space=pltpu.VMEM)] * 2,
        scratch_shapes=[pltpu.VMEM(o.shape, o.dtype)] * 4
        + [pltpu.VMEM(e.shape, e.dtype)] * 4
        + [pltpu.SemaphoreType.DMA((count,))] * 8,
        compiler_params=pltpu.CompilerParams(collective_id=1, has_side_effects=True),
        name="reduce_outputs",
    )(o, e)[0]


def stacked_heads(rows, k, group_size):
    return jnp.concatenate(
        [rows[:, (k * group_size + g) * HD : (k * group_size + g + 1) * HD] for g in range(group_size)], axis=0
    )


def scores_of(keys, query):
    return lax.dot_general(keys, query, (((1,), (1,)), ((), ())), preferred_element_type=jnp.float32)


def partial_outputs(query, blocks):
    scored = [jnp.where(mask, scores_of(keys, query), NEG_FILL) for keys, _, mask in blocks]
    peak = functools.reduce(jnp.maximum, [jnp.max(s, axis=0, keepdims=True) for s in scored])
    peak = jnp.maximum(peak, 0.1 * NEG_FILL)
    acc, total = None, None
    for s, (_, values, _) in zip(scored, blocks):
        weights = jnp.exp2((s - peak) * (SCALE * LOG2E))
        part = jnp.sum(weights, axis=0, keepdims=True)
        prod = lax.dot_general(
            values, weights.astype(jnp.bfloat16), (((0,), (0,)), ((), ())), preferred_element_type=jnp.float32
        )
        acc = prod if acc is None else acc + prod
        total = part if total is None else total + part
    empty = total == 0.0
    total = jnp.where(empty, 1.0, total)
    return acc * (1.0 / total), jnp.where(empty, NEG_FILL, peak * SCALE + jnp.log(total))


def prefill_kernel(most, heads, group_size, pages, valid, home, local, q_ref, *refs):
    page_refs, (fk_ref, fv_ref, o_ref, e_ref) = refs[:most], refs[most:]
    j = pl.program_id(0)
    rows = q_ref.shape[0]
    lanes = group_size * rows
    key_id = lax.broadcasted_iota(jnp.int32, (PAGE, 1), 0)
    fresh_id = lax.broadcasted_iota(jnp.int32, (rows, lanes), 0)
    lane_row = lax.broadcasted_iota(jnp.int32, (rows, lanes), 1) % rows
    for k in range(heads):
        cols = slice(k * HD, (k + 1) * HD)
        query = stacked_heads(q_ref, k, group_size)
        blocks = [
            (ref[0, 0, :, cols], ref[0, 1, :, cols], key_id < valid[j, i]) for i, ref in enumerate(page_refs)
        ]
        fresh_mask = (fresh_id <= lane_row) & (home[j] == 1)
        blocks.append((fk_ref[0, :, cols], fv_ref[0, :, cols], fresh_mask))
        o, e = partial_outputs(query, blocks)
        o_ref[k] = o.astype(o_ref.dtype)
        e_ref[k] = e


def decode_kernel(columns, heads, group_size, seqs, pages, valid, home, local, seq, q_ref, *refs):
    page_refs, (fk_ref, fv_ref, _, _, o_ref, e_ref) = refs[: len(columns)], refs[len(columns) :]
    j = pl.program_id(0)
    lanes = group_size * seqs
    fresh_rows = 16
    key_id = lax.broadcasted_iota(jnp.int32, (PAGE, 1), 0)
    fresh_id = lax.broadcasted_iota(jnp.int32, (fresh_rows, 1), 0)
    mine = lax.broadcasted_iota(jnp.int32, (1, lanes), 1) % seqs == seq[j]

    @pl.when(j == 0)
    def _():
        o_ref[...] = jnp.zeros_like(o_ref)
        e_ref[...] = jnp.full_like(e_ref, NEG_FILL)

    for k in range(heads):
        cols = slice(k * HD, (k + 1) * HD)
        query = stacked_heads(q_ref, k, group_size)
        blocks = [
            (ref[0, 0, :, cols], ref[0, 1, :, cols], key_id < valid[j, i]) for i, ref in zip(columns, page_refs)
        ]
        fresh_mask = fresh_id < home[j]
        blocks.append((fk_ref[0, :fresh_rows, cols], fv_ref[0, :fresh_rows, cols], fresh_mask))
        o, e = partial_outputs(query, blocks)
        place = slice(k * lanes, (k + 1) * lanes)
        o_ref[0, :, place] = jnp.where(mine, o, o_ref[0, :, place].astype(jnp.float32)).astype(o_ref.dtype)
        e_ref[0, :, place] = jnp.where(mine, e, e_ref[0, :, place])


def finish_kernel(heads, group_size, seqs, slot, flag, first, o_ref, od_ref, out_ref):
    i = pl.program_id(0)
    rows = out_ref.shape[1]

    @pl.when(flag[i] == 1)
    def _():
        for k in range(heads):
            turned = o_ref[k].astype(jnp.float32).T.astype(out_ref.dtype)
            for g in range(group_size):
                h = k * group_size + g
                out_ref[0, :, h * HD : (h + 1) * HD] = turned[g * rows : (g + 1) * rows]

    @pl.when(flag[i] != 1)
    def _():
        top = lax.broadcasted_iota(jnp.int32, (rows, 1), 0) == 0
        pick = lax.broadcasted_iota(jnp.int32, (seqs, 1), 0) == first[0] + i
        for k in range(heads):
            place = slice(k * seqs * group_size, (k + 1) * seqs * group_size)
            turned = od_ref[0, :, place].astype(jnp.float32).T
            for g in range(group_size):
                h = k * group_size + g
                line = jnp.sum(jnp.where(pick, turned[g * seqs : (g + 1) * seqs], 0.0), axis=0, keepdims=True)
                out_ref[0, :, h * HD : (h + 1) * HD] = jnp.where(top, line, 0.0).astype(out_ref.dtype)


def move_queries(queries, new_kv, kv_pages, page_table, cached_len, is_prefill):
    n = lax.axis_size("seq")
    sub_count = lax.axis_size("sub")
    z = lax.axis_index("seq")
    core = lax.axis_index("sub")
    seq_dev, row_count, query_width = queries.shape
    pages_dev, kv_width = kv_pages.shape[0], kv_pages.shape[3]
    seqs, page_count = page_table.shape
    owners = n * sub_count
    each = page_count // owners
    most = sub_count * each
    slots = seqs // 2
    group_size = query_width // kv_width
    part_width, query_part = kv_width // sub_count, query_width // sub_count
    heads = part_width // HD

    other = (core + 1) % sub_count
    away = lax.dynamic_slice_in_dim(kv_pages, other * part_width, part_width, 3)
    came = lax.ppermute(away, "sub", [(c, (c + 1) % sub_count) for c in range(sub_count)])

    seq_ids = jnp.arange(seqs, dtype=jnp.int32)
    owner = jnp.where(page_table >= 0, page_table // pages_dev, -1)
    sources = z * sub_count + jnp.stack([core, other])
    mine = owner[None] == sources[:, None, None]
    rank = jnp.cumsum(mine.astype(jnp.int32), axis=2) - 1
    picked = mine[..., None] & (rank[..., None] == jnp.arange(each, dtype=jnp.int32))
    tokens = jnp.clip(cached_len[:, None] - PAGE * jnp.arange(page_count, dtype=jnp.int32), 0, PAGE)

    def listed(values):
        found = jnp.sum(jnp.where(picked, values[None, :, :, None], 0), axis=2)
        return jnp.moveaxis(found, 0, 1).reshape(seqs, most)

    page_rows, valid_rows = listed(page_table % pages_dev), listed(tokens)
    flags = is_prefill == 1
    slot_of = jnp.cumsum(flags.astype(jnp.int32)) - 1
    place_of = jnp.cumsum((~flags).astype(jnp.int32)) - 1
    slot_ids = jnp.arange(slots, dtype=jnp.int32)
    slot_seq = jnp.sum(jnp.where(flags & (slot_of == slot_ids[:, None]), seq_ids, 0), axis=1)
    rest_ids = jnp.arange(seqs - slots, dtype=jnp.int32)
    rest_seq = jnp.sum(jnp.where(~flags & (place_of == rest_ids[:, None]), seq_ids, 0), axis=1)

    def tables(which):
        at_home = (which // seq_dev == z).astype(jnp.int32)
        places = jnp.where(at_home == 1, which % seq_dev, 0)
        chosen = which[:, None, None] == seq_ids[None, :, None]
        rows = [jnp.sum(jnp.where(chosen, x[None], 0), axis=1) for x in (page_rows, valid_rows)]
        return rows[0], rows[1], at_home, jnp.append(places, core)

    slot_tables, rest_tables = tables(slot_seq), tables(rest_seq)
    my_queries = lax.dynamic_slice_in_dim(queries, core * query_part, query_part, 2)
    own_slots = jnp.where((slot_tables[2] == 1)[:, None, None], my_queries[slot_tables[3][:slots]], 0)
    first_rows = jnp.where(
        (seq_ids // seq_dev == z)[:, None], jnp.tile(my_queries[:, 0], (n, 1)), 0
    )
    own = jnp.concatenate([own_slots.reshape(slots * row_count, query_part), first_rows], axis=0)
    gathered = gather_queries(own.astype(queries.dtype), n)

    my_fresh = lax.dynamic_slice_in_dim(new_kv, core * part_width, part_width, 3)
    fresh_keys, fresh_values = my_fresh[:, :, 0], my_fresh[:, :, 1]
    lanes = group_size * row_count
    count = slots * heads + 1

    def page_spec(i):
        if i >= each:
            return pl.BlockSpec((1, 2, PAGE, part_width), lambda j, pages, *_: (pages[j, i], 0, 0, 0))
        return pl.BlockSpec(
            (1, 2, PAGE, part_width),
            lambda j, pages, valid, home, local, *_: (pages[j, i], 0, 0, local[local.shape[0] - 1]),
        )

    fresh_spec = pl.BlockSpec(
        (1, row_count, part_width), lambda j, pages, valid, home, local, *_: (local[j], 0, 0)
    )
    o, e = pl.pallas_call(
        functools.partial(prefill_kernel, most, heads, group_size),
        grid_spec=pltpu.PrefetchScalarGridSpec(
            num_scalar_prefetch=4,
            grid=(slots,),
            in_specs=[pl.BlockSpec((row_count, query_part), lambda j, *_: (j, 0))]
            + [page_spec(i) for i in range(most)]
            + [fresh_spec] * 2,
            out_specs=[
                pl.BlockSpec((heads, HD, lanes), lambda j, *_: (j, 0, 0)),
                pl.BlockSpec((heads, 1, lanes), lambda j, *_: (j, 0, 0)),
            ],
        ),
        out_shape=[
            jax.ShapeDtypeStruct((count, HD, lanes), jnp.bfloat16),
            jax.ShapeDtypeStruct((count, 1, lanes), jnp.float32),
        ],
        name="prefill_attention",
    )(*slot_tables, gathered, *([kv_pages] * each), *([came] * (most - each)), fresh_keys, fresh_values)
    few = min(each, -(-DEC_MAXP // owners))
    columns = [*range(few), *range(each, each + few)]
    o, e = pl.pallas_call(
        functools.partial(decode_kernel, columns, heads, group_size, seqs),
        grid_spec=pltpu.PrefetchScalarGridSpec(
            num_scalar_prefetch=5,
            grid=(seqs - slots,),
            in_specs=[pl.BlockSpec((seqs, query_part), lambda j, *_: (slots * row_count // seqs, 0))]
            + [page_spec(i) for i in columns]
            + [fresh_spec] * 2
            + [pl.BlockSpec(memory_space=pl.ANY)] * 2,
            out_specs=[
                pl.BlockSpec((1, HD, lanes), lambda j, *_: (count - 1, 0, 0)),
                pl.BlockSpec((1, 1, lanes), lambda j, *_: (count - 1, 0, 0)),
            ],
        ),
        out_shape=[jax.ShapeDtypeStruct(x.shape, x.dtype) for x in (o, e)],
        input_output_aliases={8 + len(columns): 0, 9 + len(columns): 1},
        name="decode_attention",
    )(*rest_tables, rest_seq, gathered, *([kv_pages] * few), *([came] * few), fresh_keys, fresh_values, o, e)
    o = reduce_outputs(o, e, n)

    first_seq = z * seq_dev
    my_flags = lax.dynamic_slice_in_dim(is_prefill, first_seq, seq_dev, 0)
    my_slots = jnp.maximum(lax.dynamic_slice_in_dim(slot_of, first_seq, seq_dev, 0), 0)
    own_heads = pl.pallas_call(
        functools.partial(finish_kernel, heads, group_size, seqs),
        grid_spec=pltpu.PrefetchScalarGridSpec(
            num_scalar_prefetch=3,
            grid=(seq_dev,),
            in_specs=[
                pl.BlockSpec((heads, HD, lanes), lambda i, slot, *_: (slot[i], 0, 0)),
                pl.BlockSpec((1, HD, lanes), lambda i, *_: (count - 1, 0, 0)),
            ],
            out_specs=pl.BlockSpec((1, row_count, query_part), lambda i, *_: (i, 0, 0)),
        ),
        out_shape=jax.ShapeDtypeStruct((seq_dev, row_count, query_part), jnp.bfloat16),
        name="finish",
    )(my_slots, my_flags, jnp.reshape(first_seq, (1,)).astype(jnp.int32), o, o)
    pairs = [(c, (c + 1) % sub_count) for c in range(sub_count)]
    came_heads = lax.ppermute(own_heads, "sub", pairs)
    first_half = jnp.where(core == 0, own_heads, came_heads)
    second_half = jnp.where(core == 0, came_heads, own_heads)
    return jnp.concatenate([first_half, second_half], axis=2)


def per_device(queries, new_kv, kv_pages, page_table, cached_len, is_prefill):
    owners = lax.axis_size("seq") * lax.axis_size("sub")
    if page_table.shape[1] >= owners:
        return move_queries(queries, new_kv, kv_pages, page_table, cached_len, is_prefill)
    return exchange_pages(queries, new_kv, kv_pages, page_table, cached_len, is_prefill)


def solution(mesh):
    placed = (
        P(("groups", "seq"), None, "head"),
        P(("groups", "seq"), None, None, "head"),
        P(("groups", "seq", "sub"), None, None, "head"),
        P("groups", None),
        P("groups"),
        P("groups"),
    )
    return jax.shard_map(
        per_device,
        mesh=mesh,
        in_specs=placed,
        out_specs=P(("groups", "seq"), None, "head"),
        check_vma=False,
    )
```

profile of v0, /device:TPU:0, one launch (start us, length us, event | category | flops | bytes accessed | tf_op | source)
XLA Modules:
  0.0 183.9 jit_solution(4184237534698645720)
XLA Ops:
  0.0 3.8 %constant_dynamic-slice_fusion.2 = bf16[21,2,128,256]{3,2,1,0:T(8,128)(2,1)} fusion(bf16[21,2,128,512]{3,2,1,0:T(8,128)(2,1)} %refs_0_.3, s32[]{:T(128)S(6)} %select_n.182), kind=kLoop, calls=%fused_computation.54 | loop fusion | bytes 5505028 | tf_op jit(solution)/shard_map/dynamic_slice | solution.py:523
  3.8 0.5 collective-permute-start
  5.0 0.6 compare_select_fusion.2
  5.7 0.6 dynamic_slice.16.flag
  7.7 0.7 copy.22.pages
  8.3 0.7 copy.24.pages
  9.0 0.7 copy.25.valid
  9.7 0.7 copy.23.valid
  10.6 2.0 %gather_fusion = bf16[8,64,2048]{2,1,0:T(8,128)(2,1)} fusion(bf16[4,64,2048]{2,1,0:T(8,128)(2,1)S(1)} %constant_dynamic-slice_fusion.3, s32[1024]{0:T(1024)S(1)} %pad_clamp_fusion), kind=kCustom, calls=%fused_computation | custom fusion | bytes 4194336 | tf_op jit(solution)/shard_map/gather | solution.py:556
  12.7 1.8 bitcast_select_fusion
  14.5 1.6 pad_maximum_fusion
  16.0 64.8 %gather_queries.1 = bf16[33,16,2048]{2,1,0:T(8,128)(2,1)} custom-call(bf16[33,16,2048]{2,1,0:T(8,128)(2,1)} %bitcast.43), custom_call_target="tpu_custom_call" | custom-call | tf_op jit(solution)/shard_map/gather_queries/pallas_call | solution.py:285
  80.8 0.7 maximum_reduce_fusion.slot
  81.5 0.6 pad_add_fusion.local
  82.1 0.6 pad_add_fusion.1.local
  82.7 0.6 constant_dynamic-slice_fusion.1
  83.4 0.7 copy_bitcast_fusion
  84.1 15.8 %prefill_attention.1 = (bf16[17,128,512]{2,1,0:T(8,128)(2,1)}, f32[17,1,512]{2,1,0:T(1,128)}) custom-call(s32[8,4]{1,0:T(8,128)} %copy.22.pages, s32[8,4]{1,0:T(8,128)} %copy.23.valid, s32[8]{0:T(128)} %copy-done.4, s32[9]{0:T(128)} %pad_add_fusion.1.local, bf16[528,2048]{1,0:T(8,128)(2,1)} %bitcast.41, bf16[21,2,128,512]{3,2,1,0:T(8,128)(2,1)} %refs_0_.3, ...), custom_call_target="tpu_custom_call" | custom-call | tf_op jit(solution)/shard_map/prefill_attention/pallas_call | solution.py:579
  99.9 8.9 %decode_attention.1 = (bf16[17,128,512]{2,1,0:T(8,128)(2,1)}, f32[17,1,512]{2,1,0:T(1,128)}) custom-call(s32[8,4]{1,0:T(8,128)} %copy.24.pages, s32[8,4]{1,0:T(8,128)} %copy.25.valid, s32[8]{0:T(128)} %get-tuple-element.26.home, s32[9]{0:T(128)} %pad_add_fusion.local, s32[8]{0:T(128)} %copy-done.3, ...), custom_call_target="tpu_custom_call", output_to_operand_aliasing={{0}: (10, {}), {1}: (11, {})} | custom-call | tf_op jit(solution)/shard_map/decode_attention/pallas_call | solution.py:600
  108.8 65.0 %reduce_outputs.1 = (bf16[17,128,512]{2,1,0:T(8,128)(2,1)}, f32[17,1,512]{2,1,0:T(1,128)}) custom-call(bf16[17,128,512]{2,1,0:T(8,128)(2,1)} %get-tuple-element.12.o, f32[17,1,512]{2,1,0:T(1,128)} %get-tuple-element.13.e), custom_call_target="tpu_custom_call" | custom-call | tf_op jit(solution)/shard_map/reduce_outputs/pallas_call | solution.py:391
  173.8 4.3 %finish.1 = bf16[4,64,2048]{2,1,0:T(8,128)(2,1)} custom-call(s32[4]{0:T(128)} %maximum_reduce_fusion.slot, s32[4]{0:T(128)} %dynamic_slice.16.flag, s32[1]{0:T(128)} %bitcast.1.first, bf16[17,128,512]{2,1,0:T(8,128)(2,1)} %get-tuple-element.14.o_ref.od_ref, bf16[17,128,512]{2,1,0:T(8,128)(2,1)} %get-tuple-element.14.o_ref.od_ref), custom_call_target="tpu_custom_call" | custom-call | tf_op jit(solution)/shard_map/finish/pallas_call | solution.py:623
  178.1 2.9 %collective-permute-done.1 = bf16[4,64,2048]{2,1,0:T(8,128)(2,1)S(1)} collective-permute-done((bf16[4,64,2048]{2,1,0:T(8,128)(2,1)}, bf16[4,64,2048]{2,1,0:T(8,128)(2,1)S(1)}, u32[]{:S(2)}, u32[]{:S(2)}) %collective-permute-start.1) | collective-permute-done | bytes 1048608 | tf_op jit(solution)/shard_map/ppermute | solution.py:638
  181.0 1.4 broadcast_select_fusion.1
  182.4 1.5 pad_maximum_fusion.1
  (46 shorter events, 2.4 us)
Async XLA Ops:
  0.0 10.4 %copy-start = (bf16[4,64,4096]{2,1,0:T(8,128)(2,1)S(1)}, bf16[4,64,4096]{2,1,0:T(8,128)(2,1)}, u32[]{:S(2)}) copy-start(bf16[4,64,4096]{2,1,0:T(8,128)(2,1)} %param.6) | copy-start | bytes 6291460
  0.0 4.3 %copy-start.6 = (s32[16]{0:T(128)S(1)}, s32[16]{0:T(128)}, u32[]{:S(2)}) copy-start(s32[16]{0:T(128)} %param.11) | copy-start | bytes 196
  0.0 6.6 %copy-start.2 = (s32[16,16]{1,0:T(8,128)S(1)}, s32[16,16]{1,0:T(8,128)}, u32[]{:S(2)}) copy-start(s32[16,16]{1,0:T(8,128)} %param.9) | copy-start | bytes 3076
  0.0 6.6 %copy-start.5 = (s32[16]{0:T(128)S(1)}, s32[16]{0:T(128)}, u32[]{:S(2)}) copy-start(s32[16]{0:T(128)} %param.10) | copy-start | bytes 196
  3.8 80.3 %collective-permute-start = (bf16[21,2,128,256]{3,2,1,0:T(8,128)(2,1)}, bf16[21,2,128,256]{3,2,1,0:T(8,128)(2,1)}, u32[]{:S(2)}, u32[]{:S(2)}) collective-permute-start(bf16[21,2,128,256]{3,2,1,0:T(8,128)(2,1)} %constant_dynamic-slice_fusion.2), channel_id=1, source_target_pairs={{0,1},{1,0},{2,3},{3,2},{4,5},{5,4},{6,7},{7,6},{8,9},{9,8},{10,11... | collective-permute-start | bytes 8257544 | tf_op jit(solution)/shard_map/ppermute | solution.py:524
  5.0 7.6 %copy-start.3 = (s32[8]{0:T(128)}, s32[8]{0:T(128)S(1)}, u32[]{:S(2)}) copy-start(s32[8]{0:T(128)S(1)} %select_reduce_fusion.7.seq) | copy-start | bytes 100
  5.6 7.0 %copy-start.4 = (s32[8]{0:T(128)}, s32[8]{0:T(128)S(1)}, u32[]{:S(2)}) copy-start(s32[8]{0:T(128)S(1)} %get-tuple-element.42.home) | copy-start | bytes 100
  16.0 66.7 %copy-start.1 = (bf16[4,64,2,512]{3,2,1,0:T(2,128)(2,1)S(1)}, bf16[4,64,2,512]{3,2,1,0:T(2,128)(2,1)}, u32[]{:S(2)}) copy-start(bf16[4,64,2,512]{3,2,1,0:T(2,128)(2,1)} %param.7) | copy-start | bytes 1572868
  178.1 2.9 %collective-permute-start.1 = (bf16[4,64,2048]{2,1,0:T(8,128)(2,1)}, bf16[4,64,2048]{2,1,0:T(8,128)(2,1)S(1)}, u32[]{:S(2)}, u32[]{:S(2)}) collective-permute-start(bf16[4,64,2048]{2,1,0:T(8,128)(2,1)} %finish.1), channel_id=1, source_target_pairs={{0,1},{1,0},{2,3},{3,2},{4,5},{5,4},{6,7},{7,6},{8,9},{9,8},{10,11... | collective-permute-start | bytes 3145736 | tf_op jit(solution)/shard_map/ppermute | solution.py:638
where the time goes:
time: 184 us
  Pallas kernels  159 us (86%)
  local copies, waits for them, and re-layouts  11 us (6%)
  other arithmetic  10.6 us (6%)
  waiting for transfers between devices  2.87 us (2%)
    pallas_call x1, Pallas kernels, reduce_outputs(): pl.pallas_call(functools.partial(reduce_outputs_kernel, n, count), out_sh...  65 us
    pallas_call x1, Pallas kernels, gather_queries(): pl.pallas_call(functools.partial(gather_queries_kernel, n, count), out_sh...  64.8 us
    pallas_call x1, Pallas kernels, move_queries(): pl.pallas_call(functools.partial(prefill_kernel, most, heads, group_size)...  15.8 us
    pallas_call x1, Pallas kernels, move_queries(): pl.pallas_call(functools.partial(decode_kernel, columns, heads, group_siz...  8.91 us
    pallas_call x1, Pallas kernels, move_queries(): pl.pallas_call(functools.partial(finish_kernel, heads, group_size, seqs),...  4.34 us
    dynamic_slice x1, local copies, waits for them, and re-layouts, move_queries(): away = lax.dynamic_slice_in_dim(kv_pages, other * part_width, part_width, 3)  3.8 us
  transfers between devices with their start and end apart: 2, of which 1 were waited for; matrix products, arithmetic and copies ran while one was open for 8% of the time, Pallas kernels for 35%

commit v1 on v0

v1 whole, which is shorter than its diff:
```python
import functools
import itertools

import jax
import jax.numpy as jnp
from jax import lax
from jax.experimental import pallas as pl
from jax.experimental.pallas import tpu as pltpu
from jax.sharding import PartitionSpec as P

HD = 128
PAGE = 128


NEG_FILL = -1e30


def partial_softmax(
    query_heads, cache_keys, cache_values, cache_valid, fresh_keys, fresh_values, fresh_valid
):
    score_scale = HD ** (-0.5)
    cache_scores = (
        jnp.einsum("rkgd,nkd->kgrn", query_heads, cache_keys, preferred_element_type=jnp.float32)
        * score_scale
    )
    fresh_scores = (
        jnp.einsum("rkgd,jkd->kgrj", query_heads, fresh_keys, preferred_element_type=jnp.float32)
        * score_scale
    )
    cache_mask = cache_valid[None, None, None, :]
    fresh_mask = fresh_valid[None, None, :, :]
    peak = jnp.maximum(
        jnp.max(jnp.where(cache_mask, cache_scores, NEG_FILL), axis=-1),
        jnp.max(jnp.where(fresh_mask, fresh_scores, NEG_FILL), axis=-1),
    )
    cache_weights = jnp.where(cache_mask, jnp.exp(cache_scores - peak[..., None]), 0.0)
    fresh_weights = jnp.where(fresh_mask, jnp.exp(fresh_scores - peak[..., None]), 0.0)
    weight_sum = jnp.sum(cache_weights, axis=-1) + jnp.sum(fresh_weights, axis=-1)
    numerator = jnp.einsum(
        "kgrn,nkd->kgrd",
        cache_weights.astype(jnp.bfloat16),
        cache_values,
        preferred_element_type=jnp.float32,
    )
    numerator = numerator + jnp.einsum(
        "kgrj,jkd->kgrd",
        fresh_weights.astype(jnp.bfloat16),
        fresh_values,
        preferred_element_type=jnp.float32,
    )
    return (peak, weight_sum, numerator)


def attend_all(
    query_block, fresh_block, received, fetch_index, page_here, lengths, live_rows, causal, fresh_on
):
    kv_width = received.shape[-1]
    heads_kv = kv_width // HD
    row_count = query_block.shape[1]
    group_size = query_block.shape[2] // kv_width
    page_count = fetch_index.shape[1]
    positions = jnp.arange(page_count * PAGE, dtype=jnp.int32)

    def one_sequence(inputs):
        query_rows, fresh_rows, index_row, here_row, length, live_row = inputs
        fetched = jnp.take(received, index_row, axis=0)
        cache_keys = fetched[:, 0].reshape(page_count * PAGE, heads_kv, HD)
        cache_values = fetched[:, 1].reshape(page_count * PAGE, heads_kv, HD)
        page_mask = jnp.broadcast_to(here_row[:, None], (page_count, PAGE)).reshape(
            page_count * PAGE
        )
        cache_valid = page_mask & (positions < length)
        query_heads = query_rows.reshape(row_count, heads_kv, group_size, HD)
        fresh_keys = fresh_rows[:, 0].reshape(row_count, heads_kv, HD)
        fresh_values = fresh_rows[:, 1].reshape(row_count, heads_kv, HD)
        fresh_valid = causal & live_row[:, None] & fresh_on
        return partial_softmax(
            query_heads,
            cache_keys,
            cache_values,
            cache_valid,
            fresh_keys,
            fresh_values,
            fresh_valid,
        )

    return lax.map(
        one_sequence, (query_block, fresh_block, fetch_index, page_here, lengths, live_rows)
    )


def finish(weight_sum, numerator, live_rows):
    unused_rows = 1.0 - live_rows.astype(jnp.float32)
    attended = numerator / (weight_sum + unused_rows[:, None, None, :])[..., None]
    attended = jnp.where(live_rows[:, None, None, :, None], attended, 0.0)
    seq_dev, heads_kv, group_size, row_count, head_dim = attended.shape
    return (
        jnp.transpose(attended, (0, 3, 1, 2, 4))
        .reshape(seq_dev, row_count, heads_kv * group_size * head_dim)
        .astype(jnp.bfloat16)
    )


def exchange_pages(queries, new_kv, kv_pages, page_table, cached_len, is_prefill):
    seq_shards = lax.axis_size("seq")
    sub_count = lax.axis_size("sub")
    owners = seq_shards * sub_count
    seq_index = lax.axis_index("seq")
    core_index = lax.axis_index("sub")
    owner_self = seq_index * sub_count + core_index
    seq_dev, row_count, query_width = queries.shape
    pages_dev = kv_pages.shape[0]
    kv_width = kv_pages.shape[3]
    page_count = page_table.shape[1]
    entries = seq_dev * page_count
    capacity = (entries + owners - 1) // owners
    table_rows = page_table.reshape(seq_shards, entries)
    holder = jnp.where(table_rows >= 0, table_rows // pages_dev, -1)
    slot_of = jnp.where(table_rows >= 0, table_rows % pages_dev, 0)
    owned_here = holder == owner_self
    rank_among = jnp.cumsum(owned_here.astype(jnp.int32), axis=1) - 1
    picked = owned_here[:, :, None] & (
        rank_among[:, :, None] == jnp.arange(capacity, dtype=jnp.int32)[None, None, :]
    )
    send_slots = jnp.sum(jnp.where(picked, slot_of[:, :, None], 0), axis=1).reshape(
        seq_shards * capacity
    )
    first_seq = seq_index * seq_dev
    my_table = lax.dynamic_slice_in_dim(page_table, first_seq, seq_dev, 0)
    my_lengths = lax.dynamic_slice_in_dim(cached_len, first_seq, seq_dev, 0)
    my_flags = lax.dynamic_slice_in_dim(is_prefill, first_seq, seq_dev, 0)
    flat_table = my_table.reshape(entries)
    my_holder = jnp.where(flat_table >= 0, flat_table // pages_dev, -1)
    entry_order = jnp.arange(entries, dtype=jnp.int32)
    earlier = (my_holder[:, None] == my_holder[None, :]) & (
        entry_order[None, :] < entry_order[:, None]
    )
    my_rank = jnp.sum(earlier.astype(jnp.int32), axis=1)
    row_ids = jnp.arange(row_count, dtype=jnp.int32)
    live_rows = (my_flags[:, None] == 1) | (row_ids[None, :] == 0)
    causal = row_ids[None, :] <= row_ids[:, None]
    part_width = kv_width // sub_count
    split_pages = kv_pages.reshape(pages_dev, 2, PAGE, sub_count, part_width)
    chosen = jnp.take(split_pages, send_slots, axis=0).reshape(
        seq_shards, capacity, 2, PAGE, sub_count, part_width
    )
    outgoing = jnp.moveaxis(chosen, 4, 1).reshape(owners, capacity, 2, PAGE, part_width)
    received = lax.all_to_all(
        outgoing, ("seq", "sub"), split_axis=0, concat_axis=0, tiled=True
    ).reshape(owners * capacity, 2, PAGE, part_width)
    present = flat_table >= 0
    fetch_index = jnp.where(present, my_holder * capacity + my_rank, 0)
    query_part = query_width // sub_count
    my_queries = lax.dynamic_slice_in_dim(queries, core_index * query_part, query_part, 2)
    my_fresh = lax.dynamic_slice_in_dim(new_kv, core_index * part_width, part_width, 3)
    peak, weight_sum, numerator = attend_all(
        my_queries,
        my_fresh,
        received,
        fetch_index.reshape(seq_dev, page_count),
        present.reshape(seq_dev, page_count),
        my_lengths,
        live_rows,
        causal,
        core_index >= 0,
    )
    own_heads = finish(weight_sum, numerator, live_rows)
    return lax.all_gather(own_heads, "sub", axis=2, tiled=True)


MESH = pl.DeviceIdType.MESH
SCALE = HD ** (-0.5)
LOG2E = 1.4426950408889634
DEC_MAXP = 4
LANES = 256
LAG = 3
ROWS16 = 16


def hi(a, b):
    return max(a, b) if isinstance(a, int) and isinstance(b, int) else jnp.maximum(a, b)


def lo(a, b):
    return min(a, b) if isinstance(a, int) and isinstance(b, int) else jnp.minimum(a, b)


def output_bases(m, total):
    n = len(m)
    bases, before, base = [], 0, 0
    for z in range(n):
        both = lo(before, total - m[z])
        base = hi(hi(base, m[z]), both + 1 + LAG * (max(z, n - 1 - z) - z))
        bases.append(base)
        before = m[z]
    return bases


def link_lengths(n, seq_dev, slots, parts):
    total = slots * parts
    lengths = [0] * (n - 1)
    for counts in itertools.product(range(seq_dev + 1), repeat=n):
        if sum(counts) != slots or max(counts) != seq_dev:
            continue
        m = [parts * c for c in itertools.accumulate(counts)]
        bases = output_bases(m, total)
        for z in range(n - 1):
            lengths[z] = max(lengths[z], m[z], bases[z] + total - m[z] if m[z] < total else 0)
    return lengths


def pick(values, z):
    found = 0
    for j, value in enumerate(values):
        found = found + jnp.where(z == j, value, 0)
    return found


def merge(o1, e1, o2, e2):
    top = jnp.maximum(e1, e2)
    w1, w2 = jnp.exp(e1 - top), jnp.exp(e2 - top)
    total = w1 + w2
    inv = 1.0 / total
    return o1 * (w1 * inv) + o2 * (w2 * inv), top + jnp.log(total)


def attend(query, blocks):
    scored = []
    for keys, _, mask in blocks:
        s = lax.dot_general(keys, query, (((1,), (0,)), ((), ())), preferred_element_type=jnp.float32)
        scored.append(jnp.where(mask, s, NEG_FILL))
    peak = functools.reduce(jnp.maximum, [jnp.max(s, axis=0, keepdims=True) for s in scored])
    peak = jnp.maximum(peak, 0.1 * NEG_FILL)
    acc, total = None, None
    for s, (_, values, _) in zip(scored, blocks):
        weights = jnp.exp2((s - peak) * (SCALE * LOG2E))
        part = jnp.sum(weights, axis=0, keepdims=True)
        prod = lax.dot_general(
            values, weights.astype(jnp.bfloat16), (((0,), (0,)), ((), ())), preferred_element_type=jnp.float32
        )
        acc = prod if acc is None else acc + prod
        total = part if total is None else total + part
    empty = total == 0.0
    total = jnp.where(empty, 1.0, total)
    return acc * (1.0 / total), jnp.where(empty, NEG_FILL, peak * SCALE + jnp.log(total))


def fused_kernel(
    n, lengths, heads, group_size, rows, seq_dev, pages_dev,
    table, cached, flags, q_hbm, fresh, kv_hbm, out_hbm,
    kv, q_vm, own_t, out_vm, dec_rows, dec_own, dec_all, dec_o, dec_e, dec_fin,
    a_o, a_e, b_o, b_e, c_o, c_e, d_o, d_e, la_o, la_e, lc_o, lc_e, po, pe,
    dqa, dqb, dqc, dqd, doa, dea, dob, deb, doc, dec, dod, ded,
    slot_seq, rest_seq, slot_of,
    q_sem, kv_sem, kvs_sem, kvr_sem, out_sem, outs_sem, outr_sem,
    bs, br, bes, ber, ds, dr, des, der, xs, xr,
):
    z, core = lax.axis_index("seq"), lax.axis_index("sub")
    other = 1 - core
    has_left, has_right = z > 0, z < n - 1
    seqs, page_count = table.shape
    owners = 2 * n
    each = page_count // owners
    slots = seqs // 2
    rests = seqs - slots
    width = q_vm.shape[2]
    groups_part = LANES // rows
    parts_head = group_size // groups_part
    parts = heads * parts_head
    total = slots * parts
    first_seq = z * seq_dev
    dec_lanes = group_size * seqs

    q_copy = pltpu.make_async_copy(q_hbm.at[:, :, pl.ds(pl.multiple_of(core * width, width), width)], q_vm, q_sem)
    q_copy.start()

    def kv_cols(side, k):
        return kv_hbm.at[:, :, :, pl.ds(pl.multiple_of((side * heads + k) * HD, HD), HD)]

    kv_own = [pltpu.make_async_copy(kv_cols(core, k), kv.at[0, k], kv_sem.at[k]) for k in range(heads)]
    for x in kv_own:
        x.start()
    kv_far = [
        pltpu.make_async_remote_copy(
            src_ref=kv_cols(other, k), dst_ref=kv.at[1, k], send_sem=kvs_sem.at[k], recv_sem=kvr_sem.at[k],
            device_id={"sub": other}, device_id_type=MESH,
        )
        for k in range(heads)
    ]

    barrier = pltpu.get_barrier_semaphore()

    @pl.when(has_left)
    def _():
        pl.semaphore_signal(barrier, inc=1, device_id={"seq": z - 1}, device_id_type=MESH)

    @pl.when(has_right)
    def _():
        pl.semaphore_signal(barrier, inc=1, device_id={"seq": z + 1}, device_id_type=MESH)

    pl.semaphore_signal(barrier, inc=1, device_id={"sub": other}, device_id_type=MESH)

    count, cum, homes = 0, [], []
    for j in range(seqs):
        count = count + flags[j]
        cum.append(count)
        slot_of[j] = jnp.clip(count - 1, 0, slots - 1)
        if j % seq_dev == seq_dev - 1:
            homes.append(count * parts)
    for i in range(slots):
        slot_seq[i] = jnp.minimum(sum((c <= i).astype(jnp.int32) for c in cum), seqs - 1)
    for i in range(rests):
        rest_seq[i] = jnp.minimum(
            sum((j + 1 - c <= i).astype(jnp.int32) for j, c in enumerate(cum)), seqs - 1
        )
    base_r = output_bases(homes, total)
    mirrored = [total - homes[n - 2 - j] for j in range(n - 1)] + [total]
    base_l = output_bases(mirrored, total)[::-1]
    m_left, m_right = pick([0] + homes[:-1], z), pick(homes, z)
    far_left, far_right = m_left, total - m_right
    both = jnp.minimum(far_left, far_right)
    out_base_r, in_base_r = pick(base_r, z), pick([0] + base_r[:-1], z)
    out_base_l, in_base_l = pick(base_l, z), pick(base_l[1:] + [0], z)
    in_r, out_r = pick([0] + lengths, z), pick(lengths + [0], z)
    in_l, out_l = pick(lengths[::-1] + [0], z), pick([0] + lengths[::-1], z)
    top = max(lengths) - 1
    reach = LAG * jnp.maximum(z, n - 1 - z)
    dec_at = LAG * (n - 1) + rests

    def when_right(k):
        return jnp.clip(jnp.where(k < both, 2 * k, k + both), 0, total - 1)

    def when_left(k):
        return jnp.clip(jnp.where(k < both, 2 * k + 1, k + both), 0, total - 1)

    def when_own(i):
        return jnp.clip(i + far_right, 0, total - 1)

    def send(src, dst, s, r, to):
        return pltpu.make_async_remote_copy(
            src_ref=src, dst_ref=dst, send_sem=s, recv_sem=r, device_id={"seq": to}, device_id_type=MESH
        )

    def right(p):
        return (
            send(b_o.at[p], a_o.at[p], bs.at[p], br.at[p], z + 1),
            send(b_e.at[p], a_e.at[p], bes.at[p], ber.at[p], z + 1),
        )

    def left(p):
        return (
            send(d_o.at[p], c_o.at[p], ds.at[p], dr.at[p], z - 1),
            send(d_e.at[p], c_e.at[p], des.at[p], der.at[p], z - 1),
        )

    def right_dq():
        return send(dqb, dqa, xs.at[0], xr.at[0], z + 1)

    def left_dq():
        return send(dqd, dqc, xs.at[1], xr.at[1], z - 1)

    def right_do():
        return (send(dob, doa, xs.at[2], xr.at[2], z + 1), send(deb, dea, xs.at[3], xr.at[3], z + 1))

    def left_do():
        return (send(dod, doc, xs.at[4], xr.at[4], z - 1), send(ded, dec, xs.at[5], xr.at[5], z - 1))

    q_copy.wait()
    dec_rows[...] = jnp.zeros_like(dec_rows)
    for j in range(seq_dev):
        dec_rows[pl.ds(first_seq + j, 1), :] = q_vm[j, 0:ROWS16, :].astype(jnp.float32)[0:1]
    for k in range(heads):
        stacked = jnp.concatenate(
            [dec_rows[:, (k * group_size + g) * HD : (k * group_size + g + 1) * HD] for g in range(group_size)],
            axis=0,
        )
        dec_own[:, k * dec_lanes : (k + 1) * dec_lanes] = stacked.T.astype(jnp.bfloat16)

    def turn(j, carry):
        for c in range(parts):
            stacked = jnp.concatenate(
                [q_vm[j, :, (c * groups_part + g) * HD : (c * groups_part + g + 1) * HD] for g in range(groups_part)],
                axis=0,
            )
            own_t[j * parts + c] = stacked.astype(jnp.float32).T.astype(jnp.bfloat16)
        return carry

    lax.fori_loop(0, seq_dev, turn, 0)
    dec_o[...] = jnp.zeros_like(dec_o)
    dec_e[...] = jnp.full_like(dec_e, NEG_FILL)

    pl.semaphore_wait(barrier, has_left.astype(jnp.int32) + has_right.astype(jnp.int32) + 1)
    for x in kv_far:
        x.start()

    key_id = lax.broadcasted_iota(jnp.int32, (PAGE, 1), 0)
    fresh_id = lax.broadcasted_iota(jnp.int32, (rows, LANES), 0)
    lane_row = lax.broadcasted_iota(jnp.int32, (rows, LANES), 1) % rows
    causal = fresh_id <= lane_row
    dec_lane = lax.broadcasted_iota(jnp.int32, (1, heads * dec_lanes), 1) % seqs
    dec_home = dec_lane // seq_dev
    dec_seq = lax.broadcasted_iota(jnp.int32, (1, dec_lanes), 1) % seqs
    dec_fresh = lax.broadcasted_iota(jnp.int32, (ROWS16, 1), 0)

    def own_query(slot, c):
        local = jnp.clip(slot_seq[slot] - first_seq, 0, seq_dev - 1)
        return own_t[local * parts + c]

    def pages_of(seq, k, few):
        found = []
        start = table[seq, 0] // pages_dev
        for side, owner in enumerate((2 * z + core, 2 * z + other)):
            place = lax.rem(owner - start + owners, owners)
            for j in range(few):
                at = place + owners * j
                valid = jnp.clip(cached[seq] - PAGE * at, 0, PAGE)
                slot = jnp.where(valid > 0, table[seq, jnp.minimum(at, page_count - 1)] - owner * pages_dev, 0)
                slot = jnp.clip(slot, 0, pages_dev - 1)
                found.append((kv[side, k, slot, 0], kv[side, k, slot, 1], key_id < valid))
        return found

    def join(o1, e1, o2, e2, present):
        o2 = jnp.where(present, o2.astype(jnp.float32), 0.0)
        return merge(o1, e1, o2, jnp.where(present, e2, NEG_FILL))

    def assemble_right(p):
        k = jnp.clip(p - out_base_r, 0, total - 1)
        at = jnp.clip(k + in_base_r, 0, top)
        t = when_left(k)
        o, e = join(po[t], pe[t], la_o[at], la_e[at], has_left)
        q = jnp.minimum(p, total - 1)
        query = jnp.where(p < m_left, la_o[p], own_query(q // parts, q % parts))
        b_o[p] = jnp.where(p < m_right, query, o.astype(jnp.bfloat16))
        b_e[p] = e

    def assemble_left(p):
        k = jnp.clip(p - out_base_l, 0, total - 1)
        at = jnp.clip(k + in_base_l, 0, top)
        t = when_right(k)
        o, e = join(po[t], pe[t], lc_o[at], lc_e[at], has_right)
        q = jnp.minimum(p, total - 1)
        query = jnp.where(p < far_right, lc_o[p], own_query(slots - 1 - q // parts, q % parts))
        d_o[p] = jnp.where(p < total - m_left, query, o.astype(jnp.bfloat16))
        d_e[p] = e

    def compute(t):
        nearer = t - both
        apart = far_left + far_right
        paired = t < 2 * both
        is_own = t >= apart
        from_left = jnp.where(paired, t % 2 == 0, far_left > far_right)
        index = jnp.where(paired, t // 2, nearer)
        own_index = jnp.clip(t - far_right, 0, total - 1)
        index = jnp.clip(jnp.where(is_own, own_index, index), 0, total - 1)
        slot = jnp.where(is_own | from_left, index // parts, slots - 1 - index // parts)
        c = index % parts
        seq = slot_seq[slot]
        k = c // parts_head
        at = jnp.minimum(index, top)
        query = jnp.where(from_left, la_o[at], lc_o[at])
        query = jnp.where(is_own, own_query(slot, c), query)
        blocks = pages_of(seq, k, each)
        local = jnp.clip(seq - first_seq, 0, seq_dev - 1)
        head = core * heads + k
        blocks.append((fresh[local, 0, head], fresh[local, 1, head], causal & is_own))
        o, e = attend(query, blocks)
        po[t] = o
        pe[t] = e

    few = min(each, -(-DEC_MAXP // owners))

    def compute_decode(d):
        seq = rest_seq[d]
        local = jnp.clip(seq - first_seq, 0, seq_dev - 1)
        mine = dec_seq == seq
        at_home = (seq // seq_dev == z).astype(jnp.int32)
        for k in range(heads):
            cols = slice(k * dec_lanes, (k + 1) * dec_lanes)
            blocks = pages_of(seq, k, few)
            head = core * heads + k
            blocks.append(
                (fresh[local, 0, head][:ROWS16], fresh[local, 1, head][:ROWS16], dec_fresh < at_home)
            )
            o, e = attend(dec_all[:, cols], blocks)
            dec_o[:, cols] = jnp.where(mine, o, dec_o[:, cols])
            dec_e[:, cols] = jnp.where(mine, e, dec_e[:, cols])

    def step(s, carry):
        p = s - LAG * z
        w = s - LAG * (n - 1 - z)
        t = s - reach

        @pl.when(has_left & (p == 0))
        def _():
            right_dq().wait_recv()

        @pl.when(has_right & (p == 0))
        def _():
            dqb[...] = jnp.where(dec_home == z, dec_own[...], dqa[...])
            right_dq().start()

        @pl.when(has_right & (w == 0))
        def _():
            left_dq().wait_recv()

        @pl.when(has_left & (w == 0))
        def _():
            dqd[...] = jnp.where(dec_home == z, dec_own[...], dqc[...])
            left_dq().start()

        @pl.when((p >= 0) & (p < in_r))
        def _():
            for x in right(p):
                x.wait_recv()
            la_o[p] = a_o[p]
            la_e[p] = a_e[p]

        @pl.when((p >= 0) & (p < out_r))
        def _():
            assemble_right(p)
            for x in right(p):
                x.start()

        @pl.when((w >= 0) & (w < in_l))
        def _():
            for x in left(w):
                x.wait_recv()
            lc_o[w] = c_o[w]
            lc_e[w] = c_e[w]

        @pl.when((w >= 0) & (w < out_l))
        def _():
            assemble_left(w)
            for x in left(w):
                x.start()

        @pl.when(has_left & (p == dec_at))
        def _():
            for x in right_do():
                x.wait_recv()

        @pl.when(has_right & (p == dec_at))
        def _():
            o, e = join(dec_o[...], dec_e[...], doa[...], dea[...], has_left)
            dob[...] = o.astype(jnp.bfloat16)
            deb[...] = e
            for x in right_do():
                x.start()

        @pl.when(has_right & (w == dec_at))
        def _():
            for x in left_do():
                x.wait_recv()

        @pl.when(has_left & (w == dec_at))
        def _():
            o, e = join(dec_o[...], dec_e[...], doc[...], dec[...], has_right)
            dod[...] = o.astype(jnp.bfloat16)
            ded[...] = e
            for x in left_do():
                x.start()

        @pl.when(t == 0)
        def _():
            for x in kv_own:
                x.wait()
            for x in kv_far:
                x.wait_recv()
            dec_all[...] = jnp.where(dec_home < z, dqa[...], jnp.where(dec_home == z, dec_own[...], dqc[...]))

        @pl.when((t >= 0) & (t < total))
        def _():
            compute(t)

        @pl.when((t >= 0) & (t < rests))
        def _():
            compute_decode(t)

        return carry

    ends = [lengths[j] + LAG * (j + 1) for j in range(n - 1)] + [total + LAG * (n - 1)]
    ends.append(dec_at + 1 + LAG * (n - 1))
    lax.fori_loop(0, max(ends), step, 0)

    o, e = join(dec_o[...], dec_e[...], doa[...], dea[...], has_left)
    o, e = join(o, e, doc[...], dec[...], has_right)
    dec_fin[...] = o.T
    top_row = lax.broadcasted_iota(jnp.int32, (rows, 1), 0) == 0

    def out_copies(j):
        cols = pl.ds(pl.multiple_of(core * width, width), width)
        return (
            pltpu.make_async_copy(out_vm.at[j], out_hbm.at[j, :, cols], out_sem.at[j]),
            pltpu.make_async_remote_copy(
                src_ref=out_vm.at[j], dst_ref=out_hbm.at[j, :, cols], send_sem=outs_sem.at[j],
                recv_sem=outr_sem.at[j], device_id={"sub": other}, device_id_type=MESH,
            ),
        )

    def came_copies(j):
        cols = pl.ds(pl.multiple_of(other * width, width), width)
        return pltpu.make_async_remote_copy(
            src_ref=out_vm.at[j], dst_ref=out_hbm.at[j, :, cols], send_sem=outs_sem.at[j],
            recv_sem=outr_sem.at[j], device_id={"sub": other}, device_id_type=MESH,
        )

    def finish(j, carry):
        seq = first_seq + j
        chosen = flags[seq] == 1
        slot = slot_of[seq]
        for c in range(parts):
            i = slot * parts + c
            k = (slots - 1 - slot) * parts + c
            t = when_own(i)
            at_a = jnp.clip(k + in_base_r, 0, top)
            at_c = jnp.clip(i + in_base_l, 0, top)
            o, e = join(po[t], pe[t], la_o[at_a], la_e[at_a], has_left)
            o, e = join(o, e, lc_o[at_c], lc_e[at_c], has_right)
            turned = o.T
            for g in range(groups_part):
                h = c * groups_part + g
                line_at = (h // group_size) * dec_lanes + (h % group_size) * seqs + seq
                line = jnp.where(top_row, dec_fin[pl.ds(line_at, 1), :], 0.0)
                tile = jnp.where(chosen, turned[g * rows : (g + 1) * rows], line)
                out_vm[j, :, h * HD : (h + 1) * HD] = tile.astype(out_vm.dtype)
        for x in out_copies(j):
            x.start()
        return carry

    lax.fori_loop(0, seq_dev, finish, 0)

    def drain_right(p, carry):
        for x in right(p):
            x.wait_send()
        return carry

    def drain_left(p, carry):
        for x in left(p):
            x.wait_send()
        return carry

    for x in kv_far:
        x.wait_send()

    lax.fori_loop(0, out_r, drain_right, 0)
    lax.fori_loop(0, out_l, drain_left, 0)

    @pl.when(has_right)
    def _():
        right_dq().wait_send()
        for x in right_do():
            x.wait_send()

    @pl.when(has_left)
    def _():
        left_dq().wait_send()
        for x in left_do():
            x.wait_send()

    def drain_out(j, carry):
        mine, sent = out_copies(j)
        mine.wait()
        sent.wait_send()
        came_copies(j).wait_recv()
        return carry

    lax.fori_loop(0, seq_dev, drain_out, 0)


def fused_attention(queries, new_kv, kv_pages, page_table, cached_len, is_prefill):
    n = lax.axis_size("seq")
    sub_count = lax.axis_size("sub")
    seq_dev, rows, query_width = queries.shape
    pages_dev, kv_width = kv_pages.shape[0], kv_pages.shape[3]
    seqs = page_table.shape[0]
    slots = seqs // 2
    group_size = query_width // kv_width
    heads_all = kv_width // HD
    heads = heads_all // sub_count
    width = query_width // sub_count
    parts = heads * group_size * rows // LANES
    lengths = link_lengths(n, seq_dev, slots, parts)
    count, total = max(lengths), slots * parts
    fresh = jnp.transpose(new_kv.reshape(seq_dev, rows, 2, heads_all, HD), (0, 2, 3, 1, 4))
    bf, f32 = jnp.bfloat16, jnp.float32
    dec = heads * group_size * seqs

    def data(c, lanes=LANES):
        return pltpu.VMEM((c, HD, lanes), bf)

    def stat(c, lanes=LANES):
        return pltpu.VMEM((c, 1, lanes), f32)

    dma = pltpu.SemaphoreType.DMA
    scratch = [
        pltpu.VMEM((2, heads, pages_dev, 2, PAGE, HD), bf),
        pltpu.VMEM((seq_dev, rows, width), bf),
        data(seq_dev * parts),
        pltpu.VMEM((seq_dev, rows, width), bf),
        pltpu.VMEM((seqs, width), f32),
        pltpu.VMEM((HD, dec), bf),
        pltpu.VMEM((HD, dec), bf),
        pltpu.VMEM((HD, dec), f32),
        pltpu.VMEM((1, dec), f32),
        pltpu.VMEM((dec, HD), f32),
    ]
    scratch += [data(count), stat(count)] * 6
    scratch += [pltpu.VMEM((total, HD, LANES), f32), stat(total)]
    scratch += [pltpu.VMEM((HD, dec), bf)] * 4
    scratch += [pltpu.VMEM((HD, dec), bf), pltpu.VMEM((1, dec), f32)] * 4
    scratch += [pltpu.SMEM((slots,), jnp.int32), pltpu.SMEM((seqs - slots,), jnp.int32)]
    scratch += [pltpu.SMEM((seqs,), jnp.int32)]
    scratch += [dma, dma((heads,)), dma((heads,)), dma((heads,))] + [dma((seq_dev,))] * 3
    scratch += [dma((count,))] * 8 + [dma((6,))] * 2
    smem = pl.BlockSpec(memory_space=pltpu.SMEM)
    return pl.pallas_call(
        functools.partial(fused_kernel, n, lengths, heads, group_size, rows, seq_dev, pages_dev),
        out_shape=jax.ShapeDtypeStruct(queries.shape, queries.dtype),
        in_specs=[smem] * 3
        + [
            pl.BlockSpec(memory_space=pl.ANY),
            pl.BlockSpec(memory_space=pltpu.VMEM),
            pl.BlockSpec(memory_space=pl.ANY),
        ],
        out_specs=pl.BlockSpec(memory_space=pl.ANY),
        scratch_shapes=scratch,
        compiler_params=pltpu.CompilerParams(
            collective_id=0, has_side_effects=True, vmem_limit_bytes=60 * 1024 * 1024
        ),
        name="paged_attention",
    )(page_table, cached_len, is_prefill, queries, fresh, kv_pages)


def per_device(queries, new_kv, kv_pages, page_table, cached_len, is_prefill):
    owners = lax.axis_size("seq") * lax.axis_size("sub")
    if page_table.shape[1] >= owners:
        return fused_attention(queries, new_kv, kv_pages, page_table, cached_len, is_prefill)
    return exchange_pages(queries, new_kv, kv_pages, page_table, cached_len, is_prefill)


def solution(mesh):
    placed = (
        P(("groups", "seq"), None, "head"),
        P(("groups", "seq"), None, None, "head"),
        P(("groups", "seq", "sub"), None, None, "head"),
        P("groups", None),
        P("groups"),
        P("groups"),
    )
    return jax.shard_map(
        per_device,
        mesh=mesh,
        in_specs=placed,
        out_specs=P(("groups", "seq"), None, "head"),
        check_vma=False,
    )
```

time: 184 us -> 85.8 us (0.47)
  the two profiles are of different devices: /device:TPU:0 before, /device:TPU:15 now
where the time goes in v1:
time: 85.8 us; the launch traced here: 85.6 us
  Pallas kernels  80.1 us (93%)
  local copies, waits for them, and re-layouts  5.43 us (6%)
    pallas_call x1, Pallas kernels, fused_attention(): pl.pallas_call(functools.partial(fused_kernel, n, lengths, heads, group_s...  80.1 us
    unnamed x1, local copies, waits for them, and re-layouts  3.13 us
    reshape x2, local copies, waits for them, and re-layouts, fused_attention(): new_kv.reshape(seq_dev, rows, 2, heads_all, HD)  2.3 us

profile of v1, /device:TPU:15, one launch (start us, length us, event | category | flops | bytes accessed | tf_op | source)
XLA Modules:
  0.0 85.6 jit_solution(875672370842064968)
XLA Ops:
  0.0 1.4 %reshape.4 = bf16[4,64,2,4,128]{4,3,2,1,0:T(4,128)(2,1)S(1)} reshape(bf16[4,64,2,512]{3,2,1,0:T(2,128)(2,1)} %param.7) | data formatting | bytes 1048576 | tf_op jit(solution)/shard_map/reshape | solution.py:684
  1.4 0.9 %copy.12 = bf16[4,64,2,4,128]{4,1,3,2,0:T(8,128)(2,1)} copy(bf16[4,64,2,4,128]{4,3,2,1,0:T(4,128)(2,1)S(1)} %reshape.4) | data formatting | bytes 1048576 | tf_op jit(solution)/shard_map/reshape | solution.py:684
  2.3 80.1 %paged_attention.1 = bf16[4,64,4096]{2,1,0:T(8,128)(2,1)} custom-call(s32[16,16]{1,0:T(8,128)} %table.1, s32[16]{0:T(128)} %cached.1, s32[16]{0:T(128)} %flags.1, bf16[4,64,4096]{2,1,0:T(8,128)(2,1)} %q_hbm.1, bf16[4,2,4,64,128]{4,3,2,1,0:T(8,128)(2,1)} %bitcast.3, bf16[21,2,128,512]{3,2,1,0:T(8,128)(2,1)} %kv_hbm.1), custom_call_target="tpu_custom_call" | custom-call | tf_op jit(solution)/shard_map/paged_attention/pallas_call | solution.py:716
  82.4 3.1 %copy.14 = bf16[4,64,4096]{2,1,0:T(8,128)(2,1)} copy(bf16[4,64,4096]{2,1,0:T(8,128)(2,1)} %paged_attention.1) | data formatting | bytes 4194304

commit v2 on v1

--- a/solution.py
+++ b/solution.py
@@ -247,12 +247,13 @@
 
 def fused_kernel(
     n, lengths, heads, group_size, rows, seq_dev, pages_dev,
-    table, cached, flags, q_hbm, fresh, kv_hbm, out_hbm,
-    kv, q_vm, own_t, out_vm, dec_rows, dec_own, dec_all, dec_o, dec_e, dec_fin,
+    table_hbm, cached_hbm, flags_hbm, q_hbm, new_hbm, kv_hbm, out,
+    table, cached, flags, new_kv,
+    kv, q_vm, own_t, fresh, dec_rows, dec_own, dec_all, dec_o, dec_e, dec_fin,
     a_o, a_e, b_o, b_e, c_o, c_e, d_o, d_e, la_o, la_e, lc_o, lc_e, po, pe,
     dqa, dqb, dqc, dqd, doa, dea, dob, deb, doc, dec, dod, ded,
-    slot_seq, rest_seq, slot_of,
-    q_sem, kv_sem, kvs_sem, kvr_sem, out_sem, outs_sem, outr_sem,
+    slot_seq, rest_seq, slot_of, rest_of,
+    in_sem, q_sem, kv_sem, kvs_sem, kvr_sem, outs_sem, outr_sem,
     bs, br, bes, ber, ds, dr, des, der, xs, xr,
 ):
     z, core = lax.axis_index("seq"), lax.axis_index("sub")
@@ -269,8 +270,17 @@
     parts = heads * parts_head
     total = slots * parts
     first_seq = z * seq_dev
-    dec_lanes = group_size * seqs
-
+    head_lanes = group_size * rests
+    dec_lanes = heads * head_lanes
+
+    small = [
+        pltpu.make_async_copy(src, dst, in_sem.at[i])
+        for i, (src, dst) in enumerate(
+            ((table_hbm, table), (cached_hbm, cached), (flags_hbm, flags), (new_hbm, new_kv))
+        )
+    ]
+    for x in small:
+        x.start()
     q_copy = pltpu.make_async_copy(q_hbm.at[:, :, pl.ds(pl.multiple_of(core * width, width), width)], q_vm, q_sem)
     q_copy.start()
 
@@ -300,11 +310,14 @@
 
     pl.semaphore_signal(barrier, inc=1, device_id={"sub": other}, device_id_type=MESH)
 
+    for x in small[:3]:
+        x.wait()
     count, cum, homes = 0, [], []
     for j in range(seqs):
         count = count + flags[j]
         cum.append(count)
         slot_of[j] = jnp.clip(count - 1, 0, slots - 1)
+        rest_of[j] = jnp.clip(j - count, 0, rests - 1)
         if j % seq_dev == seq_dev - 1:
             homes.append(count * parts)
     for i in range(slots):
@@ -365,16 +378,20 @@
     def left_do():
         return (send(dod, doc, xs.at[4], xr.at[4], z - 1), send(ded, dec, xs.at[5], xr.at[5], z - 1))
 
+    dec_lane = lax.broadcasted_iota(jnp.int32, (1, dec_lanes), 1)
+    dec_of = dec_lane % rests
+    dec_head = dec_lane // head_lanes
+    dec_home = jnp.zeros((1, dec_lanes), jnp.int32)
     q_copy.wait()
-    dec_rows[...] = jnp.zeros_like(dec_rows)
-    for j in range(seq_dev):
-        dec_rows[pl.ds(first_seq + j, 1), :] = q_vm[j, 0:ROWS16, :].astype(jnp.float32)[0:1]
-    for k in range(heads):
-        stacked = jnp.concatenate(
-            [dec_rows[:, (k * group_size + g) * HD : (k * group_size + g + 1) * HD] for g in range(group_size)],
-            axis=0,
-        )
-        dec_own[:, k * dec_lanes : (k + 1) * dec_lanes] = stacked.T.astype(jnp.bfloat16)
+    for d in range(rests):
+        home = rest_seq[d] // seq_dev
+        local = jnp.clip(rest_seq[d] - first_seq, 0, seq_dev - 1)
+        dec_rows[d : d + 1, :] = q_vm[local, 0:ROWS16, :].astype(jnp.float32)[0:1]
+        dec_home = jnp.where(dec_of == d, home, dec_home)
+    stacked = jnp.concatenate(
+        [dec_rows[:, h * HD : (h + 1) * HD] for h in range(heads * group_size)], axis=0
+    )
+    dec_own[...] = stacked.T.astype(jnp.bfloat16)
 
     def turn(j, carry):
         for c in range(parts):
@@ -386,6 +403,11 @@
         return carry
 
     lax.fori_loop(0, seq_dev, turn, 0)
+    small[3].wait()
+    for j in range(seq_dev):
+        for t in range(2):
+            for h in range(2 * heads):
+                fresh[j, t, h] = new_kv[j, :, t, h * HD : (h + 1) * HD]
     dec_o[...] = jnp.zeros_like(dec_o)
     dec_e[...] = jnp.full_like(dec_e, NEG_FILL)
 
@@ -397,9 +419,6 @@
     fresh_id = lax.broadcasted_iota(jnp.int32, (rows, LANES), 0)
     lane_row = lax.broadcasted_iota(jnp.int32, (rows, LANES), 1) % rows
     causal = fresh_id <= lane_row
-    dec_lane = lax.broadcasted_iota(jnp.int32, (1, heads * dec_lanes), 1) % seqs
-    dec_home = dec_lane // seq_dev
-    dec_seq = lax.broadcasted_iota(jnp.int32, (1, dec_lanes), 1) % seqs
     dec_fresh = lax.broadcasted_iota(jnp.int32, (ROWS16, 1), 0)
 
     def own_query(slot, c):
@@ -472,18 +491,17 @@
     def compute_decode(d):
         seq = rest_seq[d]
         local = jnp.clip(seq - first_seq, 0, seq_dev - 1)
-        mine = dec_seq == seq
         at_home = (seq // seq_dev == z).astype(jnp.int32)
         for k in range(heads):
-            cols = slice(k * dec_lanes, (k + 1) * dec_lanes)
+            mine = (dec_of == d) & (dec_head == k)
             blocks = pages_of(seq, k, few)
             head = core * heads + k
             blocks.append(
                 (fresh[local, 0, head][:ROWS16], fresh[local, 1, head][:ROWS16], dec_fresh < at_home)
             )
-            o, e = attend(dec_all[:, cols], blocks)
-            dec_o[:, cols] = jnp.where(mine, o, dec_o[:, cols])
-            dec_e[:, cols] = jnp.where(mine, e, dec_e[:, cols])
+            o, e = attend(dec_all[...], blocks)
+            dec_o[...] = jnp.where(mine, o, dec_o[...])
+            dec_e[...] = jnp.where(mine, e, dec_e[...])
 
     def step(s, carry):
         p = s - LAG * z
@@ -587,21 +605,11 @@
     dec_fin[...] = o.T
     top_row = lax.broadcasted_iota(jnp.int32, (rows, 1), 0) == 0
 
-    def out_copies(j):
-        cols = pl.ds(pl.multiple_of(core * width, width), width)
-        return (
-            pltpu.make_async_copy(out_vm.at[j], out_hbm.at[j, :, cols], out_sem.at[j]),
-            pltpu.make_async_remote_copy(
-                src_ref=out_vm.at[j], dst_ref=out_hbm.at[j, :, cols], send_sem=outs_sem.at[j],
-                recv_sem=outr_sem.at[j], device_id={"sub": other}, device_id_type=MESH,
-            ),
-        )
-
-    def came_copies(j):
-        cols = pl.ds(pl.multiple_of(other * width, width), width)
+    def share(j, side):
+        part = out.at[j, :, pl.ds(pl.multiple_of(side * width, width), width)]
         return pltpu.make_async_remote_copy(
-            src_ref=out_vm.at[j], dst_ref=out_hbm.at[j, :, cols], send_sem=outs_sem.at[j],
-            recv_sem=outr_sem.at[j], device_id={"sub": other}, device_id_type=MESH,
+            src_ref=part, dst_ref=part, send_sem=outs_sem.at[j], recv_sem=outr_sem.at[j],
+            device_id={"sub": other}, device_id_type=MESH,
         )
 
     def finish(j, carry):
@@ -619,12 +627,12 @@
             turned = o.T
             for g in range(groups_part):
                 h = c * groups_part + g
-                line_at = (h // group_size) * dec_lanes + (h % group_size) * seqs + seq
+                line_at = h * rests + rest_of[seq]
                 line = jnp.where(top_row, dec_fin[pl.ds(line_at, 1), :], 0.0)
                 tile = jnp.where(chosen, turned[g * rows : (g + 1) * rows], line)
-                out_vm[j, :, h * HD : (h + 1) * HD] = tile.astype(out_vm.dtype)
-        for x in out_copies(j):
-            x.start()
+                place = pl.multiple_of(core * width + h * HD, HD)
+                out[j, :, pl.ds(place, HD)] = tile.astype(out.dtype)
+        share(j, core).start()
         return carry
 
     lax.fori_loop(0, seq_dev, finish, 0)
@@ -658,10 +666,8 @@
             x.wait_send()
 
     def drain_out(j, carry):
-        mine, sent = out_copies(j)
-        mine.wait()
-        sent.wait_send()
-        came_copies(j).wait_recv()
+        share(j, core).wait_send()
+        share(j, other).wait_recv()
         return carry
 
     lax.fori_loop(0, seq_dev, drain_out, 0)
@@ -681,9 +687,8 @@
     parts = heads * group_size * rows // LANES
     lengths = link_lengths(n, seq_dev, slots, parts)
     count, total = max(lengths), slots * parts
-    fresh = jnp.transpose(new_kv.reshape(seq_dev, rows, 2, heads_all, HD), (0, 2, 3, 1, 4))
     bf, f32 = jnp.bfloat16, jnp.float32
-    dec = heads * group_size * seqs
+    dec = heads * group_size * (seqs - slots)
 
     def data(c, lanes=LANES):
         return pltpu.VMEM((c, HD, lanes), bf)
@@ -693,11 +698,15 @@
 
     dma = pltpu.SemaphoreType.DMA
     scratch = [
+        pltpu.SMEM(page_table.shape, jnp.int32),
+        pltpu.SMEM(cached_len.shape, jnp.int32),
+        pltpu.SMEM(is_prefill.shape, jnp.int32),
+        pltpu.VMEM(new_kv.shape, bf),
         pltpu.VMEM((2, heads, pages_dev, 2, PAGE, HD), bf),
         pltpu.VMEM((seq_dev, rows, width), bf),
         data(seq_dev * parts),
-        pltpu.VMEM((seq_dev, rows, width), bf),
-        pltpu.VMEM((seqs, width), f32),
+        pltpu.VMEM((seq_dev, 2, heads_all, rows, HD), bf),
+        pltpu.VMEM((seqs - slots, width), f32),
         pltpu.VMEM((HD, dec), bf),
         pltpu.VMEM((HD, dec), bf),
         pltpu.VMEM((HD, dec), f32),
@@ -709,26 +718,21 @@
     scratch += [pltpu.VMEM((HD, dec), bf)] * 4
     scratch += [pltpu.VMEM((HD, dec), bf), pltpu.VMEM((1, dec), f32)] * 4
     scratch += [pltpu.SMEM((slots,), jnp.int32), pltpu.SMEM((seqs - slots,), jnp.int32)]
-    scratch += [pltpu.SMEM((seqs,), jnp.int32)]
-    scratch += [dma, dma((heads,)), dma((heads,)), dma((heads,))] + [dma((seq_dev,))] * 3
+    scratch += [pltpu.SMEM((seqs,), jnp.int32)] * 2
+    scratch += [dma((4,)), dma, dma((heads,)), dma((heads,)), dma((heads,))] + [dma((seq_dev,))] * 2
     scratch += [dma((count,))] * 8 + [dma((6,))] * 2
-    smem = pl.BlockSpec(memory_space=pltpu.SMEM)
+    operands = (page_table, cached_len, is_prefill, queries, new_kv, kv_pages)
     return pl.pallas_call(
         functools.partial(fused_kernel, n, lengths, heads, group_size, rows, seq_dev, pages_dev),
         out_shape=jax.ShapeDtypeStruct(queries.shape, queries.dtype),
-        in_specs=[smem] * 3
-        + [
-            pl.BlockSpec(memory_space=pl.ANY),
-            pl.BlockSpec(memory_space=pltpu.VMEM),
-            pl.BlockSpec(memory_space=pl.ANY),
-        ],
-        out_specs=pl.BlockSpec(memory_space=pl.ANY),
+        in_specs=[pl.BlockSpec(memory_space=pltpu.HBM)] * 6,
+        out_specs=pl.BlockSpec(memory_space=pltpu.VMEM),
         scratch_shapes=scratch,
         compiler_params=pltpu.CompilerParams(
-            collective_id=0, has_side_effects=True, vmem_limit_bytes=60 * 1024 * 1024
+            collective_id=0, has_side_effects=True, vmem_limit_bytes=48 * 1024 * 1024
         ),
         name="paged_attention",
-    )(page_table, cached_len, is_prefill, queries, fresh, kv_pages)
+    )(*[pltpu.with_memory_space_constraint(x, pltpu.HBM) for x in operands])
 
 
 def per_device(queries, new_kv, kv_pages, page_table, cached_len, is_prefill):

time: 85.8 us -> 80.6 us (0.939)
  the two profiles are of different devices: /device:TPU:15 before, /device:TPU:9 now
where the time goes in v2:
time: 80.6 us; the launch traced here: 80.4 us
  Pallas kernels  79.1 us (98%)
  local copies, waits for them, and re-layouts  1.32 us (2%)
    pallas_call x1, Pallas kernels, fused_attention(): pl.pallas_call(functools.partial(fused_kernel, n, lengths, heads, group_s...  79.1 us

profile of v2, /device:TPU:9, one launch (start us, length us, event | category | flops | bytes accessed | tf_op | source)
XLA Modules:
  0.0 80.4 jit_solution(17100496829880087778)
XLA Ops:
  0.0 79.1 %paged_attention.1 = bf16[4,64,4096]{2,1,0:T(8,128)(2,1)S(1)} custom-call(s32[16,16]{1,0:T(8,128)} %table_hbm.1, s32[16]{0:T(128)} %cached_hbm.1, s32[16]{0:T(128)} %flags_hbm.1, bf16[4,64,4096]{2,1,0:T(8,128)(2,1)} %q_hbm.1, bf16[4,64,2,512]{3,2,1,0:T(2,128)(2,1)} %new_hbm.1, bf16[21,2,128,512]{3,2,1,0:T(8,128)(2,1)} %kv_hbm.1), custom_call_target="tpu_custom_call" | custom-call | tf_op jit(solution)/shard_map/paged_attention/pallas_call | solution.py:725
  79.1 1.3 %copy.8 = bf16[4,64,4096]{2,1,0:T(8,128)(2,1)} copy(bf16[4,64,4096]{2,1,0:T(8,128)(2,1)S(1)} %paged_attention.1) | data formatting | bytes 4194304

commit v3 on v2

--- a/solution.py
+++ b/solution.py
@@ -174,6 +174,7 @@
 DEC_MAXP = 4
 LANES = 256
 LAG = 3
+FIRST = 1
 ROWS16 = 16
 
 
@@ -185,28 +186,48 @@
     return min(a, b) if isinstance(a, int) and isinstance(b, int) else jnp.minimum(a, b)
 
 
-def output_bases(m, total):
-    n = len(m)
-    bases, before, base = [], 0, 0
-    for z in range(n):
-        both = lo(before, total - m[z])
-        base = hi(hi(base, m[z]), both + 1 + LAG * (max(z, n - 1 - z) - z))
+def sel(c, a, b):
+    return (a if c else b) if isinstance(c, bool) else jnp.where(c, a, b)
+
+
+def query_spans(own):
+    spans, leads, span, lead = [], [], 0, 0
+    for count in own:
+        lead = sel(count > 0, 0, LAG + lead)
+        span = sel(span == 0, count, LAG + span + hi(count - LAG, 0))
+        spans.append(span)
+        leads.append(lead)
+    return spans, leads
+
+
+def stream_plan(own):
+    n = len(own)
+    spans, _ = query_spans(own)
+    back, back_leads = query_spans(own[::-1])
+    bases, base = [], 0
+    for z in range(n - 1):
+        ahead, behind = (spans[z - 1] if z else 0), back[n - 2 - z]
+        clear = hi(spans[z] - back_leads[n - 2 - z], lo(ahead, behind) + LAG + FIRST)
+        base = hi(base, clear)
         bases.append(base)
-        before = m[z]
-    return bases
-
-
-def link_lengths(n, seq_dev, slots, parts):
-    total = slots * parts
-    lengths = [0] * (n - 1)
+        base = base + 2 * LAG
+    return spans, bases
+
+
+def stream_lengths(n, seq_dev, slots, parts):
+    lengths, work = [0] * (n - 1), 0
     for counts in itertools.product(range(seq_dev + 1), repeat=n):
         if sum(counts) != slots or max(counts) != seq_dev:
             continue
-        m = [parts * c for c in itertools.accumulate(counts)]
-        bases = output_bases(m, total)
-        for z in range(n - 1):
-            lengths[z] = max(lengths[z], m[z], bases[z] + total - m[z] if m[z] < total else 0)
-    return lengths
+        own = [parts * c for c in counts]
+        spans, bases = stream_plan(own)
+        back = query_spans(own[::-1])[0]
+        for z in range(n):
+            ahead, behind = (spans[z - 1] if z else 0), (back[n - 2 - z] if z < n - 1 else 0)
+            work = max(work, ahead + behind + own[z])
+            if z < n - 1:
+                lengths[z] = max(lengths[z], spans[z], bases[z] + behind if behind else 0)
+    return lengths, work
 
 
 def pick(values, z):
@@ -246,13 +267,13 @@
 
 
 def fused_kernel(
-    n, lengths, heads, group_size, rows, seq_dev, pages_dev,
+    n, lengths, work, heads, group_size, rows, seq_dev, pages_dev,
     table_hbm, cached_hbm, flags_hbm, q_hbm, new_hbm, kv_hbm, out,
     table, cached, flags, new_kv,
     kv, q_vm, own_t, fresh, dec_rows, dec_own, dec_all, dec_o, dec_e, dec_fin,
     a_o, a_e, b_o, b_e, c_o, c_e, d_o, d_e, la_o, la_e, lc_o, lc_e, po, pe,
     dqa, dqb, dqc, dqd, doa, dea, dob, deb, doc, dec, dod, ded,
-    slot_seq, rest_seq, slot_of, rest_of,
+    slot_seq, rest_seq, slot_of, rest_of, own_tab, start_tab, in_tab,
     in_sem, q_sem, kv_sem, kvs_sem, kvr_sem, outs_sem, outr_sem,
     bs, br, bes, ber, ds, dr, des, der, xs, xr,
 ):
@@ -268,10 +289,21 @@
     groups_part = LANES // rows
     parts_head = group_size // groups_part
     parts = heads * parts_head
-    total = slots * parts
     first_seq = z * seq_dev
     head_lanes = group_size * rests
     dec_lanes = heads * head_lanes
+
+    barrier = pltpu.get_barrier_semaphore()
+
+    @pl.when(has_left)
+    def _():
+        pl.semaphore_signal(barrier, inc=1, device_id={"seq": z - 1}, device_id_type=MESH)
+
+    @pl.when(has_right)
+    def _():
+        pl.semaphore_signal(barrier, inc=1, device_id={"seq": z + 1}, device_id_type=MESH)
+
+    pl.semaphore_signal(barrier, inc=1, device_id={"sub": other}, device_id_type=MESH)
 
     small = [
         pltpu.make_async_copy(src, dst, in_sem.at[i])
@@ -298,42 +330,38 @@
         for k in range(heads)
     ]
 
-    barrier = pltpu.get_barrier_semaphore()
-
-    @pl.when(has_left)
-    def _():
-        pl.semaphore_signal(barrier, inc=1, device_id={"seq": z - 1}, device_id_type=MESH)
-
-    @pl.when(has_right)
-    def _():
-        pl.semaphore_signal(barrier, inc=1, device_id={"seq": z + 1}, device_id_type=MESH)
-
-    pl.semaphore_signal(barrier, inc=1, device_id={"sub": other}, device_id_type=MESH)
-
     for x in small[:3]:
         x.wait()
-    count, cum, homes = 0, [], []
+    count, cum, own, before = 0, [], [], 0
     for j in range(seqs):
         count = count + flags[j]
         cum.append(count)
         slot_of[j] = jnp.clip(count - 1, 0, slots - 1)
         rest_of[j] = jnp.clip(j - count, 0, rests - 1)
         if j % seq_dev == seq_dev - 1:
-            homes.append(count * parts)
+            start_tab[j // seq_dev] = before
+            own.append((count - before) * parts)
+            own_tab[j // seq_dev] = own[-1]
+            before = count
     for i in range(slots):
         slot_seq[i] = jnp.minimum(sum((c <= i).astype(jnp.int32) for c in cum), seqs - 1)
     for i in range(rests):
         rest_seq[i] = jnp.minimum(
             sum((j + 1 - c <= i).astype(jnp.int32) for j, c in enumerate(cum)), seqs - 1
         )
-    base_r = output_bases(homes, total)
-    mirrored = [total - homes[n - 2 - j] for j in range(n - 1)] + [total]
-    base_l = output_bases(mirrored, total)[::-1]
-    m_left, m_right = pick([0] + homes[:-1], z), pick(homes, z)
-    far_left, far_right = m_left, total - m_right
-    both = jnp.minimum(far_left, far_right)
-    out_base_r, in_base_r = pick(base_r, z), pick([0] + base_r[:-1], z)
-    out_base_l, in_base_l = pick(base_l, z), pick(base_l[1:] + [0], z)
+    spans_r, base_r = stream_plan(own)
+    spans_l, base_l = stream_plan(own[::-1])
+    ins_r, ins_l = [0] + spans_r[:-1], spans_l[::-1][1:] + [0]
+    for w in range(n):
+        in_tab[w] = ins_r[w]
+        in_tab[n + w] = ins_l[w]
+    query_in_r, query_in_l = pick(ins_r, z), pick(ins_l, z)
+    query_out_r, query_out_l = pick(spans_r, z), pick(spans_l[::-1], z)
+    both = jnp.minimum(query_in_r, query_in_l)
+    foreign = query_in_r + query_in_l
+    my_start = start_tab[z]
+    out_base_r, in_base_r = pick(base_r + [0], z), pick([0] + base_r, z)
+    out_base_l, in_base_l = pick(([0] + base_l[::-1]), z), pick(base_l[::-1] + [0], z)
     in_r, out_r = pick([0] + lengths, z), pick(lengths + [0], z)
     in_l, out_l = pick(lengths[::-1] + [0], z), pick([0] + lengths[::-1], z)
     top = max(lengths) - 1
@@ -341,13 +369,10 @@
     dec_at = LAG * (n - 1) + rests
 
     def when_right(k):
-        return jnp.clip(jnp.where(k < both, 2 * k, k + both), 0, total - 1)
+        return jnp.clip(jnp.where(k < both, 2 * k, k + both), 0, work - 1)
 
     def when_left(k):
-        return jnp.clip(jnp.where(k < both, 2 * k + 1, k + both), 0, total - 1)
-
-    def when_own(i):
-        return jnp.clip(i + far_right, 0, total - 1)
+        return jnp.clip(jnp.where(k < both, 2 * k + 1, k + both), 0, work - 1)
 
     def send(src, dst, s, r, to):
         return pltpu.make_async_remote_copy(
@@ -377,6 +402,10 @@
 
     def left_do():
         return (send(dod, doc, xs.at[4], xr.at[4], z - 1), send(ded, dec, xs.at[5], xr.at[5], z - 1))
+
+    pl.semaphore_wait(barrier, has_left.astype(jnp.int32) + has_right.astype(jnp.int32) + 1)
+    for x in kv_far:
+        x.start()
 
     dec_lane = lax.broadcasted_iota(jnp.int32, (1, dec_lanes), 1)
     dec_of = dec_lane % rests
@@ -403,17 +432,8 @@
         return carry
 
     lax.fori_loop(0, seq_dev, turn, 0)
-    small[3].wait()
-    for j in range(seq_dev):
-        for t in range(2):
-            for h in range(2 * heads):
-                fresh[j, t, h] = new_kv[j, :, t, h * HD : (h + 1) * HD]
     dec_o[...] = jnp.zeros_like(dec_o)
     dec_e[...] = jnp.full_like(dec_e, NEG_FILL)
-
-    pl.semaphore_wait(barrier, has_left.astype(jnp.int32) + has_right.astype(jnp.int32) + 1)
-    for x in kv_far:
-        x.start()
 
     key_id = lax.broadcasted_iota(jnp.int32, (PAGE, 1), 0)
     fresh_id = lax.broadcasted_iota(jnp.int32, (rows, LANES), 0)
@@ -421,9 +441,26 @@
     causal = fresh_id <= lane_row
     dec_fresh = lax.broadcasted_iota(jnp.int32, (ROWS16, 1), 0)
 
-    def own_query(slot, c):
+    def own_query(rank):
+        rank = jnp.clip(rank, 0, seq_dev * parts - 1)
+        slot = jnp.minimum(my_start + rank // parts, slots - 1)
         local = jnp.clip(slot_seq[slot] - first_seq, 0, seq_dev - 1)
-        return own_t[local * parts + c]
+        return own_t[local * parts + rank % parts]
+
+    def resolve(q, side):
+        w, home, rank, done = z - 1 + 2 * side, 0, 0, False
+        for _ in range(n - 1):
+            w = jnp.clip(w, 0, n - 1)
+            ahead = in_tab[side * n + w]
+            direct = (ahead == 0) | (q < jnp.minimum(own_tab[w], LAG))
+            hit = direct | (q >= LAG + ahead)
+            found = hit & jnp.logical_not(done)
+            home = jnp.where(found, w, home)
+            rank = jnp.where(found, jnp.where(direct, q, q - ahead), rank)
+            done = done | hit
+            q = q - LAG
+            w = w + 2 * side - 1
+        return home, jnp.clip(rank, 0, seq_dev * parts - 1)
 
     def pages_of(seq, k, few):
         found = []
@@ -443,41 +480,41 @@
         return merge(o1, e1, o2, jnp.where(present, e2, NEG_FILL))
 
     def assemble_right(p):
-        k = jnp.clip(p - out_base_r, 0, total - 1)
-        at = jnp.clip(k + in_base_r, 0, top)
+        k = jnp.maximum(p - out_base_r, 0)
+        at = jnp.clip(k + LAG + in_base_r, 0, top)
         t = when_left(k)
         o, e = join(po[t], pe[t], la_o[at], la_e[at], has_left)
-        q = jnp.minimum(p, total - 1)
-        query = jnp.where(p < m_left, la_o[p], own_query(q // parts, q % parts))
-        b_o[p] = jnp.where(p < m_right, query, o.astype(jnp.bfloat16))
+        came = (query_in_r > 0) & (p >= LAG) & (p < LAG + query_in_r)
+        mine = own_query(jnp.where((query_in_r == 0) | (p < LAG), p, p - query_in_r))
+        query = jnp.where(came, la_o[jnp.clip(p - LAG, 0, top)], mine)
+        b_o[p] = jnp.where(p < query_out_r, query, o.astype(jnp.bfloat16))
         b_e[p] = e
 
     def assemble_left(p):
-        k = jnp.clip(p - out_base_l, 0, total - 1)
-        at = jnp.clip(k + in_base_l, 0, top)
+        k = jnp.maximum(p - out_base_l, 0)
+        at = jnp.clip(k + LAG + in_base_l, 0, top)
         t = when_right(k)
         o, e = join(po[t], pe[t], lc_o[at], lc_e[at], has_right)
-        q = jnp.minimum(p, total - 1)
-        query = jnp.where(p < far_right, lc_o[p], own_query(slots - 1 - q // parts, q % parts))
-        d_o[p] = jnp.where(p < total - m_left, query, o.astype(jnp.bfloat16))
+        came = (query_in_l > 0) & (p >= LAG) & (p < LAG + query_in_l)
+        mine = own_query(jnp.where((query_in_l == 0) | (p < LAG), p, p - query_in_l))
+        query = jnp.where(came, lc_o[jnp.clip(p - LAG, 0, top)], mine)
+        d_o[p] = jnp.where(p < query_out_l, query, o.astype(jnp.bfloat16))
         d_e[p] = e
 
     def compute(t):
-        nearer = t - both
-        apart = far_left + far_right
         paired = t < 2 * both
-        is_own = t >= apart
-        from_left = jnp.where(paired, t % 2 == 0, far_left > far_right)
-        index = jnp.where(paired, t // 2, nearer)
-        own_index = jnp.clip(t - far_right, 0, total - 1)
-        index = jnp.clip(jnp.where(is_own, own_index, index), 0, total - 1)
-        slot = jnp.where(is_own | from_left, index // parts, slots - 1 - index // parts)
-        c = index % parts
-        seq = slot_seq[slot]
-        k = c // parts_head
-        at = jnp.minimum(index, top)
-        query = jnp.where(from_left, la_o[at], lc_o[at])
-        query = jnp.where(is_own, own_query(slot, c), query)
+        is_own = t >= foreign
+        right_more = query_in_r <= query_in_l
+        side = jnp.where(paired, t % 2, right_more.astype(jnp.int32))
+        index = jnp.clip(jnp.where(paired, t // 2, t - both), 0, top)
+        home, rank = resolve(index, side)
+        home = jnp.where(is_own, z, home)
+        own_rank = jnp.clip(t - foreign, 0, seq_dev * parts - 1)
+        rank = jnp.where(is_own, own_rank, rank)
+        seq = slot_seq[jnp.minimum(start_tab[home] + rank // parts, slots - 1)]
+        k = (rank % parts) // parts_head
+        query = jnp.where(side == 0, la_o[index], lc_o[index])
+        query = jnp.where(is_own, own_query(own_rank), query)
         blocks = pages_of(seq, k, each)
         local = jnp.clip(seq - first_seq, 0, seq_dev - 1)
         head = core * heads + k
@@ -504,9 +541,8 @@
             dec_e[...] = jnp.where(mine, e, dec_e[...])
 
     def step(s, carry):
-        p = s - LAG * z
-        w = s - LAG * (n - 1 - z)
-        t = s - reach
+        p, w = s - LAG * z, s - LAG * (n - 1 - z)
+        t, d, r = s - LAG, s - reach, s - LAG
 
         @pl.when(has_left & (p == 0))
         def _():
@@ -526,30 +562,30 @@
             dqd[...] = jnp.where(dec_home == z, dec_own[...], dqc[...])
             left_dq().start()
 
-        @pl.when((p >= 0) & (p < in_r))
-        def _():
-            for x in right(p):
+        @pl.when((r >= 0) & (r < in_r))
+        def _():
+            for x in right(r):
                 x.wait_recv()
-            la_o[p] = a_o[p]
-            la_e[p] = a_e[p]
-
-        @pl.when((p >= 0) & (p < out_r))
-        def _():
-            assemble_right(p)
-            for x in right(p):
+            la_o[r] = a_o[r]
+            la_e[r] = a_e[r]
+
+        @pl.when(s < out_r)
+        def _():
+            assemble_right(s)
+            for x in right(s):
                 x.start()
 
-        @pl.when((w >= 0) & (w < in_l))
-        def _():
-            for x in left(w):
+        @pl.when((r >= 0) & (r < in_l))
+        def _():
+            for x in left(r):
                 x.wait_recv()
-            lc_o[w] = c_o[w]
-            lc_e[w] = c_e[w]
-
-        @pl.when((w >= 0) & (w < out_l))
-        def _():
-            assemble_left(w)
-            for x in left(w):
+            lc_o[r] = c_o[r]
+            lc_e[r] = c_e[r]
+
+        @pl.when(s < out_l)
+        def _():
+            assemble_left(s)
+            for x in left(s):
                 x.start()
 
         @pl.when(has_left & (p == dec_at))
@@ -584,21 +620,30 @@
                 x.wait()
             for x in kv_far:
                 x.wait_recv()
+            small[3].wait()
+
+        @pl.when((t >= 0) & (t < seq_dev))
+        def _():
+            for i in range(2):
+                for h in range(2 * heads):
+                    fresh[t, i, h] = new_kv[t, :, i, h * HD : (h + 1) * HD]
+
+        @pl.when((t >= 0) & (t < work))
+        def _():
+            compute(t)
+
+        @pl.when(d == 0)
+        def _():
             dec_all[...] = jnp.where(dec_home < z, dqa[...], jnp.where(dec_home == z, dec_own[...], dqc[...]))
 
-        @pl.when((t >= 0) & (t < total))
-        def _():
-            compute(t)
-
-        @pl.when((t >= 0) & (t < rests))
-        def _():
-            compute_decode(t)
+        @pl.when((d >= 0) & (d < rests))
+        def _():
+            compute_decode(d)
 
         return carry
 
-    ends = [lengths[j] + LAG * (j + 1) for j in range(n - 1)] + [total + LAG * (n - 1)]
-    ends.append(dec_at + 1 + LAG * (n - 1))
-    lax.fori_loop(0, max(ends), step, 0)
+    steps = max(max(lengths) + LAG, work + LAG, dec_at + 1 + LAG * (n - 1))
+    lax.fori_loop(0, steps, step, 0)
 
     o, e = join(dec_o[...], dec_e[...], doa[...], dea[...], has_left)
     o, e = join(o, e, doc[...], dec[...], has_right)
@@ -617,11 +662,12 @@
         chosen = flags[seq] == 1
         slot = slot_of[seq]
         for c in range(parts):
-            i = slot * parts + c
-            k = (slots - 1 - slot) * parts + c
-            t = when_own(i)
-            at_a = jnp.clip(k + in_base_r, 0, top)
-            at_c = jnp.clip(i + in_base_l, 0, top)
+            rank = jnp.maximum((slot - my_start) * parts + c, 0)
+            t = jnp.minimum(foreign + rank, work - 1)
+            to_left = jnp.where((query_in_l == 0) | (rank < LAG), rank, rank + query_in_l)
+            to_right = jnp.where((query_in_r == 0) | (rank < LAG), rank, rank + query_in_r)
+            at_a = jnp.clip(to_left + in_base_r, 0, top)
+            at_c = jnp.clip(to_right + in_base_l, 0, top)
             o, e = join(po[t], pe[t], la_o[at_a], la_e[at_a], has_left)
             o, e = join(o, e, lc_o[at_c], lc_e[at_c], has_right)
             turned = o.T
@@ -685,8 +731,8 @@
     heads = heads_all // sub_count
     width = query_width // sub_count
     parts = heads * group_size * rows // LANES
-    lengths = link_lengths(n, seq_dev, slots, parts)
-    count, total = max(lengths), slots * parts
+    lengths, work = stream_lengths(n, seq_dev, slots, parts)
+    count = max(lengths)
     bf, f32 = jnp.bfloat16, jnp.float32
     dec = heads * group_size * (seqs - slots)
 
@@ -714,16 +760,17 @@
         pltpu.VMEM((dec, HD), f32),
     ]
     scratch += [data(count), stat(count)] * 6
-    scratch += [pltpu.VMEM((total, HD, LANES), f32), stat(total)]
+    scratch += [pltpu.VMEM((work, HD, LANES), f32), stat(work)]
     scratch += [pltpu.VMEM((HD, dec), bf)] * 4
     scratch += [pltpu.VMEM((HD, dec), bf), pltpu.VMEM((1, dec), f32)] * 4
     scratch += [pltpu.SMEM((slots,), jnp.int32), pltpu.SMEM((seqs - slots,), jnp.int32)]
     scratch += [pltpu.SMEM((seqs,), jnp.int32)] * 2
+    scratch += [pltpu.SMEM((n,), jnp.int32)] * 2 + [pltpu.SMEM((2 * n,), jnp.int32)]
     scratch += [dma((4,)), dma, dma((heads,)), dma((heads,)), dma((heads,))] + [dma((seq_dev,))] * 2
     scratch += [dma((count,))] * 8 + [dma((6,))] * 2
     operands = (page_table, cached_len, is_prefill, queries, new_kv, kv_pages)
     return pl.pallas_call(
-        functools.partial(fused_kernel, n, lengths, heads, group_size, rows, seq_dev, pages_dev),
+        functools.partial(fused_kernel, n, lengths, work, heads, group_size, rows, seq_dev, pages_dev),
         out_shape=jax.ShapeDtypeStruct(queries.shape, queries.dtype),
         in_specs=[pl.BlockSpec(memory_space=pltpu.HBM)] * 6,
         out_specs=pl.BlockSpec(memory_space=pltpu.VMEM),

time: 80.6 us -> 77.8 us (0.965)
  the two profiles are of different devices: /device:TPU:9 before, /device:TPU:0 now
where the time goes in v3:
time: 77.8 us; the launch traced here: 77.6 us
  Pallas kernels  76.2 us (98%)
  local copies, waits for them, and re-layouts  1.32 us (2%)
    pallas_call x1, Pallas kernels, fused_attention(): pl.pallas_call(functools.partial(fused_kernel, n, lengths, work, heads, g...  76.2 us

profile of v3, /device:TPU:0, one launch (start us, length us, event | category | flops | bytes accessed | tf_op | source)
XLA Modules:
  0.0 77.6 jit_solution(2227903217502598951)
XLA Ops:
  0.0 76.2 %paged_attention.1 = bf16[4,64,4096]{2,1,0:T(8,128)(2,1)S(1)} custom-call(s32[16,16]{1,0:T(8,128)} %table_hbm.1, s32[16]{0:T(128)} %cached_hbm.1, s32[16]{0:T(128)} %flags_hbm.1, bf16[4,64,4096]{2,1,0:T(8,128)(2,1)} %q_hbm.1, bf16[4,64,2,512]{3,2,1,0:T(2,128)(2,1)} %new_hbm.1, bf16[21,2,128,512]{3,2,1,0:T(8,128)(2,1)} %kv_hbm.1), custom_call_target="tpu_custom_call" | custom-call | tf_op jit(solution)/shard_map/paged_attention/pallas_call | solution.py:772
  76.2 1.3 %copy.8 = bf16[4,64,4096]{2,1,0:T(8,128)(2,1)} copy(bf16[4,64,4096]{2,1,0:T(8,128)(2,1)S(1)} %paged_attention.1) | data formatting | bytes 4194304

commit v4 on v3

--- a/solution.py
+++ b/solution.py
@@ -366,7 +366,7 @@
     in_l, out_l = pick(lengths[::-1] + [0], z), pick([0] + lengths[::-1], z)
     top = max(lengths) - 1
     reach = LAG * jnp.maximum(z, n - 1 - z)
-    dec_at = LAG * (n - 1) + rests
+    dec_at = LAG * (n - 1) + rests * heads
 
     def when_right(k):
         return jnp.clip(jnp.where(k < both, 2 * k, k + both), 0, work - 1)
@@ -525,20 +525,18 @@
 
     few = min(each, -(-DEC_MAXP // owners))
 
-    def compute_decode(d):
+    def compute_decode(i):
+        d, k = i // heads, i % heads
         seq = rest_seq[d]
         local = jnp.clip(seq - first_seq, 0, seq_dev - 1)
         at_home = (seq // seq_dev == z).astype(jnp.int32)
-        for k in range(heads):
-            mine = (dec_of == d) & (dec_head == k)
-            blocks = pages_of(seq, k, few)
-            head = core * heads + k
-            blocks.append(
-                (fresh[local, 0, head][:ROWS16], fresh[local, 1, head][:ROWS16], dec_fresh < at_home)
-            )
-            o, e = attend(dec_all[...], blocks)
-            dec_o[...] = jnp.where(mine, o, dec_o[...])
-            dec_e[...] = jnp.where(mine, e, dec_e[...])
+        mine = (dec_of == d) & (dec_head == k)
+        blocks = pages_of(seq, k, few)
+        head = core * heads + k
+        blocks.append((fresh[local, 0, head][:ROWS16], fresh[local, 1, head][:ROWS16], dec_fresh < at_home))
+        o, e = attend(dec_all[...], blocks)
+        dec_o[...] = jnp.where(mine, o, dec_o[...])
+        dec_e[...] = jnp.where(mine, e, dec_e[...])
 
     def step(s, carry):
         p, w = s - LAG * z, s - LAG * (n - 1 - z)
@@ -636,7 +634,7 @@
         def _():
             dec_all[...] = jnp.where(dec_home < z, dqa[...], jnp.where(dec_home == z, dec_own[...], dqc[...]))
 
-        @pl.when((d >= 0) & (d < rests))
+        @pl.when((d >= 0) & (d < rests * heads))
         def _():
             compute_decode(d)
 

time: 77.8 us -> 76.2 us (0.979)
  Pallas kernels: 76.2 us -> 74.7 us
    pallas_call x1, Pallas kernels: 76.2 us -> 74.7 us  [fused_attention(): pl.pallas_call(functools.partial(fused_kernel, n, lengths, work, heads, g...]
where the time goes in v4:
time: 76.2 us; the launch traced here: 76 us
  Pallas kernels  74.7 us (98%)
  local copies, waits for them, and re-layouts  1.32 us (2%)
    pallas_call x1, Pallas kernels, fused_attention(): pl.pallas_call(functools.partial(fused_kernel, n, lengths, work, heads, g...  74.7 us

profile of v4, /device:TPU:0, one launch (start us, length us, event | category | flops | bytes accessed | tf_op | source)
XLA Modules:
  0.0 76.0 jit_solution(17443317609216363338)
XLA Ops:
  0.0 74.7 %paged_attention.1 = bf16[4,64,4096]{2,1,0:T(8,128)(2,1)S(1)} custom-call(s32[16,16]{1,0:T(8,128)} %table_hbm.1, s32[16]{0:T(128)} %cached_hbm.1, s32[16]{0:T(128)} %flags_hbm.1, bf16[4,64,4096]{2,1,0:T(8,128)(2,1)} %q_hbm.1, bf16[4,64,2,512]{3,2,1,0:T(2,128)(2,1)} %new_hbm.1, bf16[21,2,128,512]{3,2,1,0:T(8,128)(2,1)} %kv_hbm.1), custom_call_target="tpu_custom_call" | custom-call | tf_op jit(solution)/shard_map/paged_attention/pallas_call | solution.py:770
  74.7 1.3 %copy.8 = bf16[4,64,4096]{2,1,0:T(8,128)(2,1)} copy(bf16[4,64,4096]{2,1,0:T(8,128)(2,1)S(1)} %paged_attention.1) | data formatting | bytes 4194304

commit v5 on v4

--- a/solution.py
+++ b/solution.py
@@ -215,19 +215,29 @@
 
 
 def stream_lengths(n, seq_dev, slots, parts):
-    lengths, work = [0] * (n - 1), 0
+    lengths, work, ready = [0] * (n - 1), 0, [0] * seq_dev
     for counts in itertools.product(range(seq_dev + 1), repeat=n):
         if sum(counts) != slots or max(counts) != seq_dev:
             continue
         own = [parts * c for c in counts]
         spans, bases = stream_plan(own)
-        back = query_spans(own[::-1])[0]
+        back, back_bases = stream_plan(own[::-1])
         for z in range(n):
             ahead, behind = (spans[z - 1] if z else 0), (back[n - 2 - z] if z < n - 1 else 0)
+            for k in range(own[z]):
+                done = [LAG + 1 + ahead + behind + k]
+                if z:
+                    done.append(LAG + bases[z - 1] + (k if behind == 0 or k < LAG else k + behind))
+                if z < n - 1:
+                    done.append(LAG + back_bases[n - 2 - z] + (k if ahead == 0 or k < LAG else k + ahead))
+                for j in range(k // parts, seq_dev):
+                    ready[j] = max(ready[j], *done)
             work = max(work, ahead + behind + own[z])
             if z < n - 1:
                 lengths[z] = max(lengths[z], spans[z], bases[z] + behind if behind else 0)
-    return lengths, work
+    for j in range(1, seq_dev):
+        ready[j] = max(ready[j], ready[j - 1] + 1)
+    return lengths, work, ready
 
 
 def pick(values, z):
@@ -267,7 +277,7 @@
 
 
 def fused_kernel(
-    n, lengths, work, heads, group_size, rows, seq_dev, pages_dev,
+    n, lengths, work, ready, heads, group_size, rows, seq_dev, pages_dev,
     table_hbm, cached_hbm, flags_hbm, q_hbm, new_hbm, kv_hbm, out,
     table, cached, flags, new_kv,
     kv, q_vm, own_t, fresh, dec_rows, dec_own, dec_all, dec_o, dec_e, dec_fin,
@@ -311,17 +321,21 @@
             ((table_hbm, table), (cached_hbm, cached), (flags_hbm, flags), (new_hbm, new_kv))
         )
     ]
-    for x in small:
+    for x in small[:3]:
         x.start()
-    q_copy = pltpu.make_async_copy(q_hbm.at[:, :, pl.ds(pl.multiple_of(core * width, width), width)], q_vm, q_sem)
-    q_copy.start()
+    q_copy = [
+        pltpu.make_async_copy(
+            q_hbm.at[j, :, pl.ds(pl.multiple_of(core * width, width), width)], q_vm.at[j], q_sem.at[j]
+        )
+        for j in range(seq_dev)
+    ]
+    for x in q_copy:
+        x.start()
 
     def kv_cols(side, k):
         return kv_hbm.at[:, :, :, pl.ds(pl.multiple_of((side * heads + k) * HD, HD), HD)]
 
     kv_own = [pltpu.make_async_copy(kv_cols(core, k), kv.at[0, k], kv_sem.at[k]) for k in range(heads)]
-    for x in kv_own:
-        x.start()
     kv_far = [
         pltpu.make_async_remote_copy(
             src_ref=kv_cols(other, k), dst_ref=kv.at[1, k], send_sem=kvs_sem.at[k], recv_sem=kvr_sem.at[k],
@@ -367,6 +381,8 @@
     top = max(lengths) - 1
     reach = LAG * jnp.maximum(z, n - 1 - z)
     dec_at = LAG * (n - 1) + rests * heads
+    dec_done = dec_at + LAG * (n - 1)
+    ready = [max(at, dec_done + 1 + j) for j, at in enumerate(ready)]
 
     def when_right(k):
         return jnp.clip(jnp.where(k < both, 2 * k, k + both), 0, work - 1)
@@ -411,7 +427,17 @@
     dec_of = dec_lane % rests
     dec_head = dec_lane // head_lanes
     dec_home = jnp.zeros((1, dec_lanes), jnp.int32)
-    q_copy.wait()
+    for j in range(seq_dev):
+        q_copy[j].wait()
+        for c in range(parts):
+            stacked = jnp.concatenate(
+                [q_vm[j, :, (c * groups_part + g) * HD : (c * groups_part + g + 1) * HD] for g in range(groups_part)],
+                axis=0,
+            )
+            own_t[j * parts + c] = stacked.astype(jnp.float32).T.astype(jnp.bfloat16)
+    for x in kv_own:
+        x.start()
+    small[3].start()
     for d in range(rests):
         home = rest_seq[d] // seq_dev
         local = jnp.clip(rest_seq[d] - first_seq, 0, seq_dev - 1)
@@ -422,16 +448,6 @@
     )
     dec_own[...] = stacked.T.astype(jnp.bfloat16)
 
-    def turn(j, carry):
-        for c in range(parts):
-            stacked = jnp.concatenate(
-                [q_vm[j, :, (c * groups_part + g) * HD : (c * groups_part + g + 1) * HD] for g in range(groups_part)],
-                axis=0,
-            )
-            own_t[j * parts + c] = stacked.astype(jnp.float32).T.astype(jnp.bfloat16)
-        return carry
-
-    lax.fori_loop(0, seq_dev, turn, 0)
     dec_o[...] = jnp.zeros_like(dec_o)
     dec_e[...] = jnp.full_like(dec_e, NEG_FILL)
 
@@ -538,114 +554,6 @@
         dec_o[...] = jnp.where(mine, o, dec_o[...])
         dec_e[...] = jnp.where(mine, e, dec_e[...])
 
-    def step(s, carry):
-        p, w = s - LAG * z, s - LAG * (n - 1 - z)
-        t, d, r = s - LAG, s - reach, s - LAG
-
-        @pl.when(has_left & (p == 0))
-        def _():
-            right_dq().wait_recv()
-
-        @pl.when(has_right & (p == 0))
-        def _():
-            dqb[...] = jnp.where(dec_home == z, dec_own[...], dqa[...])
-            right_dq().start()
-
-        @pl.when(has_right & (w == 0))
-        def _():
-            left_dq().wait_recv()
-
-        @pl.when(has_left & (w == 0))
-        def _():
-            dqd[...] = jnp.where(dec_home == z, dec_own[...], dqc[...])
-            left_dq().start()
-
-        @pl.when((r >= 0) & (r < in_r))
-        def _():
-            for x in right(r):
-                x.wait_recv()
-            la_o[r] = a_o[r]
-            la_e[r] = a_e[r]
-
-        @pl.when(s < out_r)
-        def _():
-            assemble_right(s)
-            for x in right(s):
-                x.start()
-
-        @pl.when((r >= 0) & (r < in_l))
-        def _():
-            for x in left(r):
-                x.wait_recv()
-            lc_o[r] = c_o[r]
-            lc_e[r] = c_e[r]
-
-        @pl.when(s < out_l)
-        def _():
-            assemble_left(s)
-            for x in left(s):
-                x.start()
-
-        @pl.when(has_left & (p == dec_at))
-        def _():
-            for x in right_do():
-                x.wait_recv()
-
-        @pl.when(has_right & (p == dec_at))
-        def _():
-            o, e = join(dec_o[...], dec_e[...], doa[...], dea[...], has_left)
-            dob[...] = o.astype(jnp.bfloat16)
-            deb[...] = e
-            for x in right_do():
-                x.start()
-
-        @pl.when(has_right & (w == dec_at))
-        def _():
-            for x in left_do():
-                x.wait_recv()
-
-        @pl.when(has_left & (w == dec_at))
-        def _():
-            o, e = join(dec_o[...], dec_e[...], doc[...], dec[...], has_right)
-            dod[...] = o.astype(jnp.bfloat16)
-            ded[...] = e
-            for x in left_do():
-                x.start()
-
-        @pl.when(t == 0)
-        def _():
-            for x in kv_own:
-                x.wait()
-            for x in kv_far:
-                x.wait_recv()
-            small[3].wait()
-
-        @pl.when((t >= 0) & (t < seq_dev))
-        def _():
-            for i in range(2):
-                for h in range(2 * heads):
-                    fresh[t, i, h] = new_kv[t, :, i, h * HD : (h + 1) * HD]
-
-        @pl.when((t >= 0) & (t < work))
-        def _():
-            compute(t)
-
-        @pl.when(d == 0)
-        def _():
-            dec_all[...] = jnp.where(dec_home < z, dqa[...], jnp.where(dec_home == z, dec_own[...], dqc[...]))
-
-        @pl.when((d >= 0) & (d < rests * heads))
-        def _():
-            compute_decode(d)
-
-        return carry
-
-    steps = max(max(lengths) + LAG, work + LAG, dec_at + 1 + LAG * (n - 1))
-    lax.fori_loop(0, steps, step, 0)
-
-    o, e = join(dec_o[...], dec_e[...], doa[...], dea[...], has_left)
-    o, e = join(o, e, doc[...], dec[...], has_right)
-    dec_fin[...] = o.T
     top_row = lax.broadcasted_iota(jnp.int32, (rows, 1), 0) == 0
 
     def share(j, side):
@@ -655,7 +563,7 @@
             device_id={"sub": other}, device_id_type=MESH,
         )
 
-    def finish(j, carry):
+    def finish(j):
         seq = first_seq + j
         chosen = flags[seq] == 1
         slot = slot_of[seq]
@@ -677,9 +585,122 @@
                 place = pl.multiple_of(core * width + h * HD, HD)
                 out[j, :, pl.ds(place, HD)] = tile.astype(out.dtype)
         share(j, core).start()
+
+    def step(s, carry):
+        p, w = s - LAG * z, s - LAG * (n - 1 - z)
+        t, d, r = s - LAG, s - reach, s - LAG
+
+        @pl.when(has_left & (p == 0))
+        def _():
+            right_dq().wait_recv()
+
+        @pl.when(has_right & (p == 0))
+        def _():
+            dqb[...] = jnp.where(dec_home == z, dec_own[...], dqa[...])
+            right_dq().start()
+
+        @pl.when(has_right & (w == 0))
+        def _():
+            left_dq().wait_recv()
+
+        @pl.when(has_left & (w == 0))
+        def _():
+            dqd[...] = jnp.where(dec_home == z, dec_own[...], dqc[...])
+            left_dq().start()
+
+        @pl.when((r >= 0) & (r < in_r))
+        def _():
+            for x in right(r):
+                x.wait_recv()
+            la_o[r] = a_o[r]
+            la_e[r] = a_e[r]
+
+        @pl.when(s < out_r)
+        def _():
+            assemble_right(s)
+            for x in right(s):
+                x.start()
+
+        @pl.when((r >= 0) & (r < in_l))
+        def _():
+            for x in left(r):
+                x.wait_recv()
+            lc_o[r] = c_o[r]
+            lc_e[r] = c_e[r]
+
+        @pl.when(s < out_l)
+        def _():
+            assemble_left(s)
+            for x in left(s):
+                x.start()
+
+        @pl.when(has_left & (p == dec_at))
+        def _():
+            for x in right_do():
+                x.wait_recv()
+
+        @pl.when(has_right & (p == dec_at))
+        def _():
+            o, e = join(dec_o[...], dec_e[...], doa[...], dea[...], has_left)
+            dob[...] = o.astype(jnp.bfloat16)
+            deb[...] = e
+            for x in right_do():
+                x.start()
+
+        @pl.when(has_right & (w == dec_at))
+        def _():
+            for x in left_do():
+                x.wait_recv()
+
+        @pl.when(has_left & (w == dec_at))
+        def _():
+            o, e = join(dec_o[...], dec_e[...], doc[...], dec[...], has_right)
+            dod[...] = o.astype(jnp.bfloat16)
+            ded[...] = e
+            for x in left_do():
+                x.start()
+
+        @pl.when(t == 0)
+        def _():
+            for x in kv_own:
+                x.wait()
+            for x in kv_far:
+                x.wait_recv()
+            small[3].wait()
+
+        @pl.when((t >= 0) & (t < seq_dev))
+        def _():
+            for i in range(2):
+                for h in range(2 * heads):
+                    fresh[t, i, h] = new_kv[t, :, i, h * HD : (h + 1) * HD]
+
+        @pl.when((t >= 0) & (t < work))
+        def _():
+            compute(t)
+
+        @pl.when(d == 0)
+        def _():
+            dec_all[...] = jnp.where(dec_home < z, dqa[...], jnp.where(dec_home == z, dec_own[...], dqc[...]))
+
+        @pl.when((d >= 0) & (d < rests * heads))
+        def _():
+            compute_decode(d)
+
+        @pl.when(s == dec_done)
+        def _():
+            o, e = join(dec_o[...], dec_e[...], doa[...], dea[...], has_left)
+            o, e = join(o, e, doc[...], dec[...], has_right)
+            dec_fin[...] = o.T
+
+        @pl.when(functools.reduce(jnp.logical_or, [s == at for at in ready]))
+        def _():
+            finish(sum((s > at).astype(jnp.int32) for at in ready[:-1]))
+
         return carry
 
-    lax.fori_loop(0, seq_dev, finish, 0)
+    steps = max(max(lengths) + LAG, work + LAG, dec_done + 1, ready[-1] + 1)
+    lax.fori_loop(0, steps, step, 0)
+
 
     def drain_right(p, carry):
         for x in right(p):
@@ -729,7 +750,7 @@
     heads = heads_all // sub_count
     width = query_width // sub_count
     parts = heads * group_size * rows // LANES
-    lengths, work = stream_lengths(n, seq_dev, slots, parts)
+    lengths, work, ready = stream_lengths(n, seq_dev, slots, parts)
     count = max(lengths)
     bf, f32 = jnp.bfloat16, jnp.float32
     dec = heads * group_size * (seqs - slots)
@@ -764,11 +785,11 @@
     scratch += [pltpu.SMEM((slots,), jnp.int32), pltpu.SMEM((seqs - slots,), jnp.int32)]
     scratch += [pltpu.SMEM((seqs,), jnp.int32)] * 2
     scratch += [pltpu.SMEM((n,), jnp.int32)] * 2 + [pltpu.SMEM((2 * n,), jnp.int32)]
-    scratch += [dma((4,)), dma, dma((heads,)), dma((heads,)), dma((heads,))] + [dma((seq_dev,))] * 2
+    scratch += [dma((4,)), dma((seq_dev,)), dma((heads,)), dma((heads,)), dma((heads,))] + [dma((seq_dev,))] * 2
     scratch += [dma((count,))] * 8 + [dma((6,))] * 2
     operands = (page_table, cached_len, is_prefill, queries, new_kv, kv_pages)
     return pl.pallas_call(
-        functools.partial(fused_kernel, n, lengths, work, heads, group_size, rows, seq_dev, pages_dev),
+        functools.partial(fused_kernel, n, lengths, work, ready, heads, group_size, rows, seq_dev, pages_dev),
         out_shape=jax.ShapeDtypeStruct(queries.shape, queries.dtype),
         in_specs=[pl.BlockSpec(memory_space=pltpu.HBM)] * 6,
         out_specs=pl.BlockSpec(memory_space=pltpu.VMEM),

time: 76.2 us -> 74.4 us (0.976)
  Pallas kernels: 74.7 us -> 73 us
    pallas_call x1, Pallas kernels: 74.7 us -> 73 us  [fused_attention(): pl.pallas_call(functools.partial(fused_kernel, n, lengths, work, ready, h...]
where the time goes in v5:
time: 74.4 us; the launch traced here: 74.3 us
  Pallas kernels  73 us (98%)
  local copies, waits for them, and re-layouts  1.32 us (2%)
    pallas_call x1, Pallas kernels, fused_attention(): pl.pallas_call(functools.partial(fused_kernel, n, lengths, work, ready, h...  73 us

profile of v5, /device:TPU:0, one launch (start us, length us, event | category | flops | bytes accessed | tf_op | source)
XLA Modules:
  0.0 74.3 jit_solution(5028779538502243993)
XLA Ops:
  0.0 73.0 %paged_attention.1 = bf16[4,64,4096]{2,1,0:T(8,128)(2,1)S(1)} custom-call(s32[16,16]{1,0:T(8,128)} %table_hbm.1, s32[16]{0:T(128)} %cached_hbm.1, s32[16]{0:T(128)} %flags_hbm.1, bf16[4,64,4096]{2,1,0:T(8,128)(2,1)} %q_hbm.1, bf16[4,64,2,512]{3,2,1,0:T(2,128)(2,1)} %new_hbm.1, bf16[21,2,128,512]{3,2,1,0:T(8,128)(2,1)} %kv_hbm.1), custom_call_target="tpu_custom_call" | custom-call | tf_op jit(solution)/shard_map/paged_attention/pallas_call | solution.py:791
  73.0 1.3 %copy.8 = bf16[4,64,4096]{2,1,0:T(8,128)(2,1)} copy(bf16[4,64,4096]{2,1,0:T(8,128)(2,1)S(1)} %paged_attention.1) | data formatting | bytes 4194304

commit v6 on v5

--- a/solution.py
+++ b/solution.py
@@ -174,7 +174,6 @@
 DEC_MAXP = 4
 LANES = 256
 LAG = 3
-FIRST = 1
 ROWS16 = 16
 
 
@@ -200,14 +199,32 @@
     return spans, leads
 
 
+def work_order(ahead, lead_a, behind, lead_b):
+    a, b = sel(ahead == 0, 0, lead_a), sel(behind == 0, 0, lead_b)
+    swap = b >= a
+    early, late = sel(swap, ahead, behind), sel(swap, behind, ahead)
+    skip = lo(sel(swap, b - a, a - b), early)
+    both = hi(lo(early - skip, late - skip), 0)
+    delay = sel(b > a, sel(late - skip > both, both, hi(both - 1, 0)), both)
+    return swap, skip, both, early + late - skip, delay
+
+
+def chip_order(own, z):
+    n = len(own)
+    spans, leads = query_spans(own)
+    back, back_leads = query_spans(own[::-1])
+    ahead = (spans[z - 1], leads[z - 1]) if z else (0, 0)
+    behind = (back[n - 2 - z], back_leads[n - 2 - z]) if z < n - 1 else (0, 0)
+    return work_order(*ahead, *behind)
+
+
 def stream_plan(own):
     n = len(own)
     spans, _ = query_spans(own)
     back, back_leads = query_spans(own[::-1])
     bases, base = [], 0
     for z in range(n - 1):
-        ahead, behind = (spans[z - 1] if z else 0), back[n - 2 - z]
-        clear = hi(spans[z] - back_leads[n - 2 - z], lo(ahead, behind) + LAG + FIRST)
+        clear = hi(spans[z] - back_leads[n - 2 - z], chip_order(own, z)[4] + LAG + (1 if z else 0))
         base = hi(base, clear)
         bases.append(base)
         base = base + 2 * LAG
@@ -224,15 +241,16 @@
         back, back_bases = stream_plan(own[::-1])
         for z in range(n):
             ahead, behind = (spans[z - 1] if z else 0), (back[n - 2 - z] if z < n - 1 else 0)
+            foreign = chip_order(own, z)[3]
             for k in range(own[z]):
-                done = [LAG + 1 + ahead + behind + k]
+                done = [LAG + 1 + foreign + k]
                 if z:
                     done.append(LAG + bases[z - 1] + (k if behind == 0 or k < LAG else k + behind))
                 if z < n - 1:
                     done.append(LAG + back_bases[n - 2 - z] + (k if ahead == 0 or k < LAG else k + ahead))
                 for j in range(k // parts, seq_dev):
                     ready[j] = max(ready[j], *done)
-            work = max(work, ahead + behind + own[z])
+            work = max(work, chip_order(own, z)[3] + own[z])
             if z < n - 1:
                 lengths[z] = max(lengths[z], spans[z], bases[z] + behind if behind else 0)
     for j in range(1, seq_dev):
@@ -371,8 +389,9 @@
         in_tab[n + w] = ins_l[w]
     query_in_r, query_in_l = pick(ins_r, z), pick(ins_l, z)
     query_out_r, query_out_l = pick(spans_r, z), pick(spans_l[::-1], z)
-    both = jnp.minimum(query_in_r, query_in_l)
-    foreign = query_in_r + query_in_l
+    orders = [chip_order(own, w) for w in range(n)]
+    left_late = pick([jnp.asarray(x[0]).astype(jnp.int32) for x in orders], z) == 1
+    skip, both, foreign = (pick([x[i] for x in orders], z) for i in (1, 2, 3))
     my_start = start_tab[z]
     out_base_r, in_base_r = pick(base_r + [0], z), pick([0] + base_r, z)
     out_base_l, in_base_l = pick(([0] + base_l[::-1]), z), pick(base_l[::-1] + [0], z)
@@ -384,11 +403,11 @@
     dec_done = dec_at + LAG * (n - 1)
     ready = [max(at, dec_done + 1 + j) for j, at in enumerate(ready)]
 
-    def when_right(k):
-        return jnp.clip(jnp.where(k < both, 2 * k, k + both), 0, work - 1)
-
-    def when_left(k):
-        return jnp.clip(jnp.where(k < both, 2 * k + 1, k + both), 0, work - 1)
+    def when(k, late):
+        i = k - skip
+        paired = skip + 2 * i + jnp.where(late, 0, 1)
+        at = jnp.where(i < both, paired, skip + both + i)
+        return jnp.clip(jnp.where(i < 0, k, at), 0, work - 1)
 
     def send(src, dst, s, r, to):
         return pltpu.make_async_remote_copy(
@@ -498,7 +517,7 @@
     def assemble_right(p):
         k = jnp.maximum(p - out_base_r, 0)
         at = jnp.clip(k + LAG + in_base_r, 0, top)
-        t = when_left(k)
+        t = when(k, left_late)
         o, e = join(po[t], pe[t], la_o[at], la_e[at], has_left)
         came = (query_in_r > 0) & (p >= LAG) & (p < LAG + query_in_r)
         mine = own_query(jnp.where((query_in_r == 0) | (p < LAG), p, p - query_in_r))
@@ -509,7 +528,7 @@
     def assemble_left(p):
         k = jnp.maximum(p - out_base_l, 0)
         at = jnp.clip(k + LAG + in_base_l, 0, top)
-        t = when_right(k)
+        t = when(k, jnp.logical_not(left_late))
         o, e = join(po[t], pe[t], lc_o[at], lc_e[at], has_right)
         came = (query_in_l > 0) & (p >= LAG) & (p < LAG + query_in_l)
         mine = own_query(jnp.where((query_in_l == 0) | (p < LAG), p, p - query_in_l))
@@ -518,11 +537,12 @@
         d_e[p] = e
 
     def compute(t):
-        paired = t < 2 * both
+        i = t - skip
         is_own = t >= foreign
-        right_more = query_in_r <= query_in_l
-        side = jnp.where(paired, t % 2, right_more.astype(jnp.int32))
-        index = jnp.clip(jnp.where(paired, t // 2, t - both), 0, top)
+        from_late = jnp.where(i < 2 * both, i % 2 == 0, left_late == (query_in_l > query_in_r)) & (i >= 0)
+        side = (from_late == left_late).astype(jnp.int32)
+        index = jnp.where(i < 0, t, skip + jnp.where(i < 2 * both, i // 2, i - both))
+        index = jnp.clip(index, 0, top)
         home, rank = resolve(index, side)
         home = jnp.where(is_own, z, home)
         own_rank = jnp.clip(t - foreign, 0, seq_dev * parts - 1)
@@ -586,6 +606,8 @@
                 out[j, :, pl.ds(place, HD)] = tile.astype(out.dtype)
         share(j, core).start()
 
+    middle = has_left & has_right
+
     def step(s, carry):
         p, w = s - LAG * z, s - LAG * (n - 1 - z)
         t, d, r = s - LAG, s - reach, s - LAG
@@ -615,13 +637,32 @@
             la_o[r] = a_o[r]
             la_e[r] = a_e[r]
 
+        @pl.when(jnp.logical_not(has_left) & (r >= 0) & (r < in_l))
+        def _():
+            for x in left(r):
+                x.wait_recv()
+            lc_o[r] = c_o[r]
+            lc_e[r] = c_e[r]
+
+        @pl.when(jnp.logical_not(middle) & (t == 0))
+        def _():
+            for x in kv_own:
+                x.wait()
+            for x in kv_far:
+                x.wait_recv()
+            small[3].wait()
+
+        @pl.when(jnp.logical_not(middle) & (t >= 0) & (t < work))
+        def _():
+            compute(t)
+
         @pl.when(s < out_r)
         def _():
             assemble_right(s)
             for x in right(s):
                 x.start()
 
-        @pl.when((r >= 0) & (r < in_l))
+        @pl.when(has_left & (r >= 0) & (r < in_l))
         def _():
             for x in left(r):
                 x.wait_recv()
@@ -660,7 +701,7 @@
             for x in left_do():
                 x.start()
 
-        @pl.when(t == 0)
+        @pl.when(middle & (t == 0))
         def _():
             for x in kv_own:
                 x.wait()
@@ -674,7 +715,7 @@
                 for h in range(2 * heads):
                     fresh[t, i, h] = new_kv[t, :, i, h * HD : (h + 1) * HD]
 
-        @pl.when((t >= 0) & (t < work))
+        @pl.when(middle & (t >= 0) & (t < work))
         def _():
             compute(t)
 

time: 74.4 us -> 73 us (0.981)
  Pallas kernels: 73 us -> 71.5 us
    pallas_call x1, Pallas kernels: 73 us -> 71.5 us  [fused_attention(): pl.pallas_call(functools.partial(fused_kernel, n, lengths, work, ready, h...]
where the time goes in v6:
time: 73 us; the launch traced here: 72.8 us
  Pallas kernels  71.5 us (98%)
  local copies, waits for them, and re-layouts  1.32 us (2%)
    pallas_call x1, Pallas kernels, fused_attention(): pl.pallas_call(functools.partial(fused_kernel, n, lengths, work, ready, h...  71.5 us

profile of v6, /device:TPU:0, one launch (start us, length us, event | category | flops | bytes accessed | tf_op | source)
XLA Modules:
  0.0 72.8 jit_solution(9842779175104164292)
XLA Ops:
  0.0 71.5 %paged_attention.1 = bf16[4,64,4096]{2,1,0:T(8,128)(2,1)S(1)} custom-call(s32[16,16]{1,0:T(8,128)} %table_hbm.1, s32[16]{0:T(128)} %cached_hbm.1, s32[16]{0:T(128)} %flags_hbm.1, bf16[4,64,4096]{2,1,0:T(8,128)(2,1)} %q_hbm.1, bf16[4,64,2,512]{3,2,1,0:T(2,128)(2,1)} %new_hbm.1, bf16[21,2,128,512]{3,2,1,0:T(8,128)(2,1)} %kv_hbm.1), custom_call_target="tpu_custom_call" | custom-call | tf_op jit(solution)/shard_map/paged_attention/pallas_call | solution.py:832
  71.5 1.3 %copy.8 = bf16[4,64,4096]{2,1,0:T(8,128)(2,1)} copy(bf16[4,64,4096]{2,1,0:T(8,128)(2,1)S(1)} %paged_attention.1) | data formatting | bytes 4194304

commit v7 on v6

--- a/solution.py
+++ b/solution.py
@@ -400,7 +400,7 @@
     top = max(lengths) - 1
     reach = LAG * jnp.maximum(z, n - 1 - z)
     dec_at = LAG * (n - 1) + rests * heads
-    dec_done = dec_at + LAG * (n - 1)
+    dec_done = dec_at + 1 + LAG * (n - 1)
     ready = [max(at, dec_done + 1 + j) for j, at in enumerate(ready)]
 
     def when(k, late):
@@ -458,14 +458,7 @@
         x.start()
     small[3].start()
     for d in range(rests):
-        home = rest_seq[d] // seq_dev
-        local = jnp.clip(rest_seq[d] - first_seq, 0, seq_dev - 1)
-        dec_rows[d : d + 1, :] = q_vm[local, 0:ROWS16, :].astype(jnp.float32)[0:1]
-        dec_home = jnp.where(dec_of == d, home, dec_home)
-    stacked = jnp.concatenate(
-        [dec_rows[:, h * HD : (h + 1) * HD] for h in range(heads * group_size)], axis=0
-    )
-    dec_own[...] = stacked.T.astype(jnp.bfloat16)
+        dec_home = jnp.where(dec_of == d, rest_seq[d] // seq_dev, dec_home)
 
     dec_o[...] = jnp.zeros_like(dec_o)
     dec_e[...] = jnp.full_like(dec_e, NEG_FILL)
@@ -609,8 +602,8 @@
     middle = has_left & has_right
 
     def step(s, carry):
-        p, w = s - LAG * z, s - LAG * (n - 1 - z)
-        t, d, r = s - LAG, s - reach, s - LAG
+        p, w = s - 1 - LAG * z, s - 1 - LAG * (n - 1 - z)
+        t, d, r = s - LAG, s - 1 - reach, s - LAG
 
         @pl.when(has_left & (p == 0))
         def _():
@@ -650,7 +643,6 @@
                 x.wait()
             for x in kv_far:
                 x.wait_recv()
-            small[3].wait()
 
         @pl.when(jnp.logical_not(middle) & (t >= 0) & (t < work))
         def _():
@@ -707,17 +699,28 @@
                 x.wait()
             for x in kv_far:
                 x.wait_recv()
+
+        @pl.when(s == LAG - 1)
+        def _():
             small[3].wait()
-
-        @pl.when((t >= 0) & (t < seq_dev))
-        def _():
-            for i in range(2):
-                for h in range(2 * heads):
-                    fresh[t, i, h] = new_kv[t, :, i, h * HD : (h + 1) * HD]
+            for j in range(seq_dev):
+                for i in range(2):
+                    for h in range(2 * heads):
+                        fresh[j, i, h] = new_kv[j, :, i, h * HD : (h + 1) * HD]
 
         @pl.when(middle & (t >= 0) & (t < work))
         def _():
             compute(t)
+
+        @pl.when(s == 0)
+        def _():
+            for d in range(rests):
+                local = jnp.clip(rest_seq[d] - first_seq, 0, seq_dev - 1)
+                dec_rows[d : d + 1, :] = q_vm[local, 0:ROWS16, :].astype(jnp.float32)[0:1]
+            stacked = jnp.concatenate(
+                [dec_rows[:, h * HD : (h + 1) * HD] for h in range(heads * group_size)], axis=0
+            )
+            dec_own[...] = stacked.T.astype(jnp.bfloat16)
 
         @pl.when(d == 0)
         def _():

time: 73 us -> 72.5 us (level)
  no operation moved by 1% of the time
where the time goes in v7:
time: 72.5 us; the launch traced here: 72.3 us
  Pallas kernels  71 us (98%)
  local copies, waits for them, and re-layouts  1.32 us (2%)
    pallas_call x1, Pallas kernels, fused_attention(): pl.pallas_call(functools.partial(fused_kernel, n, lengths, work, ready, h...  71 us

profile of v7, /device:TPU:0, one launch (start us, length us, event | category | flops | bytes accessed | tf_op | source)
XLA Modules:
  0.0 72.3 jit_solution(14501052665011457397)
XLA Ops:
  0.0 71.0 %paged_attention.1 = bf16[4,64,4096]{2,1,0:T(8,128)(2,1)S(1)} custom-call(s32[16,16]{1,0:T(8,128)} %table_hbm.1, s32[16]{0:T(128)} %cached_hbm.1, s32[16]{0:T(128)} %flags_hbm.1, bf16[4,64,4096]{2,1,0:T(8,128)(2,1)} %q_hbm.1, bf16[4,64,2,512]{3,2,1,0:T(2,128)(2,1)} %new_hbm.1, bf16[21,2,128,512]{3,2,1,0:T(8,128)(2,1)} %kv_hbm.1), custom_call_target="tpu_custom_call" | custom-call | tf_op jit(solution)/shard_map/paged_attention/pallas_call | solution.py:835
  71.0 1.3 %copy.8 = bf16[4,64,4096]{2,1,0:T(8,128)(2,1)} copy(bf16[4,64,4096]{2,1,0:T(8,128)(2,1)S(1)} %paged_attention.1) | data formatting | bytes 4194304

commit v8 on v7

--- a/solution.py
+++ b/solution.py
@@ -341,14 +341,15 @@
     ]
     for x in small[:3]:
         x.start()
-    q_copy = [
-        pltpu.make_async_copy(
-            q_hbm.at[j, :, pl.ds(pl.multiple_of(core * width, width), width)], q_vm.at[j], q_sem.at[j]
-        )
-        for j in range(seq_dev)
-    ]
-    for x in q_copy:
-        x.start()
+    piece = groups_part * HD
+
+    def q_piece(c):
+        src = pl.ds(pl.multiple_of(core * width + c * piece, piece), piece)
+        dst = pl.ds(pl.multiple_of(c * piece, piece), piece)
+        return pltpu.make_async_copy(q_hbm.at[:, :, src], q_vm.at[:, :, dst], q_sem.at[c])
+
+    for c in range(parts):
+        q_piece(c).start()
 
     def kv_cols(side, k):
         return kv_hbm.at[:, :, :, pl.ds(pl.multiple_of((side * heads + k) * HD, HD), HD)]
@@ -400,7 +401,7 @@
     top = max(lengths) - 1
     reach = LAG * jnp.maximum(z, n - 1 - z)
     dec_at = LAG * (n - 1) + rests * heads
-    dec_done = dec_at + 1 + LAG * (n - 1)
+    dec_done = dec_at + parts - 1 + LAG * (n - 1)
     ready = [max(at, dec_done + 1 + j) for j, at in enumerate(ready)]
 
     def when(k, late):
@@ -446,14 +447,16 @@
     dec_of = dec_lane % rests
     dec_head = dec_lane // head_lanes
     dec_home = jnp.zeros((1, dec_lanes), jnp.int32)
-    for j in range(seq_dev):
-        q_copy[j].wait()
-        for c in range(parts):
+    def turn(c):
+        q_piece(c).wait()
+        for j in range(seq_dev):
             stacked = jnp.concatenate(
-                [q_vm[j, :, (c * groups_part + g) * HD : (c * groups_part + g + 1) * HD] for g in range(groups_part)],
+                [q_vm[j, :, pl.ds(pl.multiple_of(c * piece + g * HD, HD), HD)] for g in range(groups_part)],
                 axis=0,
             )
             own_t[j * parts + c] = stacked.astype(jnp.float32).T.astype(jnp.bfloat16)
+
+    turn(0)
     for x in kv_own:
         x.start()
     small[3].start()
@@ -602,8 +605,8 @@
     middle = has_left & has_right
 
     def step(s, carry):
-        p, w = s - 1 - LAG * z, s - 1 - LAG * (n - 1 - z)
-        t, d, r = s - LAG, s - 1 - reach, s - LAG
+        p, w = s - parts + 1 - LAG * z, s - parts + 1 - LAG * (n - 1 - z)
+        t, d, r = s - LAG, s - parts + 1 - reach, s - LAG
 
         @pl.when(has_left & (p == 0))
         def _():
@@ -700,19 +703,11 @@
             for x in kv_far:
                 x.wait_recv()
 
-        @pl.when(s == LAG - 1)
-        def _():
-            small[3].wait()
-            for j in range(seq_dev):
-                for i in range(2):
-                    for h in range(2 * heads):
-                        fresh[j, i, h] = new_kv[j, :, i, h * HD : (h + 1) * HD]
-
-        @pl.when(middle & (t >= 0) & (t < work))
-        def _():
-            compute(t)
-
-        @pl.when(s == 0)
+        @pl.when(s < parts - 1)
+        def _():
+            turn(s + 1)
+
+        @pl.when(s == parts - 2)
         def _():
             for d in range(rests):
                 local = jnp.clip(rest_seq[d] - first_seq, 0, seq_dev - 1)
@@ -721,6 +716,18 @@
                 [dec_rows[:, h * HD : (h + 1) * HD] for h in range(heads * group_size)], axis=0
             )
             dec_own[...] = stacked.T.astype(jnp.bfloat16)
+
+        @pl.when(s == LAG - 1)
+        def _():
+            small[3].wait()
+            for j in range(seq_dev):
+                for i in range(2):
+                    for h in range(2 * heads):
+                        fresh[j, i, h] = new_kv[j, :, i, h * HD : (h + 1) * HD]
+
+        @pl.when(middle & (t >= 0) & (t < work))
+        def _():
+            compute(t)
 
         @pl.when(d == 0)
         def _():
@@ -829,7 +836,7 @@
     scratch += [pltpu.SMEM((slots,), jnp.int32), pltpu.SMEM((seqs - slots,), jnp.int32)]
     scratch += [pltpu.SMEM((seqs,), jnp.int32)] * 2
     scratch += [pltpu.SMEM((n,), jnp.int32)] * 2 + [pltpu.SMEM((2 * n,), jnp.int32)]
-    scratch += [dma((4,)), dma((seq_dev,)), dma((heads,)), dma((heads,)), dma((heads,))] + [dma((seq_dev,))] * 2
+    scratch += [dma((4,)), dma((parts,)), dma((heads,)), dma((heads,)), dma((heads,))] + [dma((seq_dev,))] * 2
     scratch += [dma((count,))] * 8 + [dma((6,))] * 2
     operands = (page_table, cached_len, is_prefill, queries, new_kv, kv_pages)
     return pl.pallas_call(

time: 72.5 us -> 72 us (level)
  no operation moved by 1% of the time
where the time goes in v8:
time: 72 us; the launch traced here: 71.9 us
  Pallas kernels  70.5 us (98%)
  local copies, waits for them, and re-layouts  1.32 us (2%)
    pallas_call x1, Pallas kernels, fused_attention(): pl.pallas_call(functools.partial(fused_kernel, n, lengths, work, ready, h...  70.5 us

profile of v8, /device:TPU:0, one launch (start us, length us, event | category | flops | bytes accessed | tf_op | source)
XLA Modules:
  0.0 71.9 jit_solution(17015312487967574569)
XLA Ops:
  0.0 70.5 %paged_attention.1 = bf16[4,64,4096]{2,1,0:T(8,128)(2,1)S(1)} custom-call(s32[16,16]{1,0:T(8,128)} %table_hbm.1, s32[16]{0:T(128)} %cached_hbm.1, s32[16]{0:T(128)} %flags_hbm.1, bf16[4,64,4096]{2,1,0:T(8,128)(2,1)} %q_hbm.1, bf16[4,64,2,512]{3,2,1,0:T(2,128)(2,1)} %new_hbm.1, bf16[21,2,128,512]{3,2,1,0:T(8,128)(2,1)} %kv_hbm.1), custom_call_target="tpu_custom_call" | custom-call | tf_op jit(solution)/shard_map/paged_attention/pallas_call | solution.py:842
  70.5 1.3 %copy.8 = bf16[4,64,4096]{2,1,0:T(8,128)(2,1)} copy(bf16[4,64,4096]{2,1,0:T(8,128)(2,1)S(1)} %paged_attention.1) | data formatting | bytes 4194304

commit v9 on v8

--- a/solution.py
+++ b/solution.py
@@ -233,6 +233,7 @@
 
 def stream_lengths(n, seq_dev, slots, parts):
     lengths, work, ready = [0] * (n - 1), 0, [0] * seq_dev
+    quiet = [LAG * slots * parts] * (n - 1)
     for counts in itertools.product(range(seq_dev + 1), repeat=n):
         if sum(counts) != slots or max(counts) != seq_dev:
             continue
@@ -251,11 +252,13 @@
                 for j in range(k // parts, seq_dev):
                     ready[j] = max(ready[j], *done)
             work = max(work, chip_order(own, z)[3] + own[z])
+            if z < n - 1 and behind:
+                quiet[z] = min(quiet[z], bases[z])
             if z < n - 1:
                 lengths[z] = max(lengths[z], spans[z], bases[z] + behind if behind else 0)
     for j in range(1, seq_dev):
         ready[j] = max(ready[j], ready[j - 1] + 1)
-    return lengths, work, ready
+    return lengths, work, ready, quiet
 
 
 def pick(values, z):
@@ -295,7 +298,7 @@
 
 
 def fused_kernel(
-    n, lengths, work, ready, heads, group_size, rows, seq_dev, pages_dev,
+    n, lengths, work, ready, quiet, heads, group_size, rows, seq_dev, pages_dev,
     table_hbm, cached_hbm, flags_hbm, q_hbm, new_hbm, kv_hbm, out,
     table, cached, flags, new_kv,
     kv, q_vm, own_t, fresh, dec_rows, dec_own, dec_all, dec_o, dec_e, dec_fin,
@@ -398,6 +401,8 @@
     out_base_l, in_base_l = pick(([0] + base_l[::-1]), z), pick(base_l[::-1] + [0], z)
     in_r, out_r = pick([0] + lengths, z), pick(lengths + [0], z)
     in_l, out_l = pick(lengths[::-1] + [0], z), pick([0] + lengths[::-1], z)
+    quiet_in_r, quiet_out_r = pick([0] + quiet, z), pick(quiet + [0], z)
+    quiet_in_l, quiet_out_l = pick(quiet[::-1] + [0], z), pick([0] + quiet[::-1], z)
     top = max(lengths) - 1
     reach = LAG * jnp.maximum(z, n - 1 - z)
     dec_at = LAG * (n - 1) + rests * heads
@@ -457,8 +462,7 @@
             own_t[j * parts + c] = stacked.astype(jnp.float32).T.astype(jnp.bfloat16)
 
     turn(0)
-    for x in kv_own:
-        x.start()
+    kv_own[0].start()
     small[3].start()
     for d in range(rests):
         dec_home = jnp.where(dec_of == d, rest_seq[d] // seq_dev, dec_home)
@@ -628,17 +632,23 @@
 
         @pl.when((r >= 0) & (r < in_r))
         def _():
-            for x in right(r):
-                x.wait_recv()
+            right(r)[0].wait_recv()
             la_o[r] = a_o[r]
-            la_e[r] = a_e[r]
+
+            @pl.when(r >= quiet_in_r)
+            def _():
+                right(r)[1].wait_recv()
+                la_e[r] = a_e[r]
 
         @pl.when(jnp.logical_not(has_left) & (r >= 0) & (r < in_l))
         def _():
-            for x in left(r):
-                x.wait_recv()
+            left(r)[0].wait_recv()
             lc_o[r] = c_o[r]
-            lc_e[r] = c_e[r]
+
+            @pl.when(r >= quiet_in_l)
+            def _():
+                left(r)[1].wait_recv()
+                lc_e[r] = c_e[r]
 
         @pl.when(jnp.logical_not(middle) & (t == 0))
         def _():
@@ -654,21 +664,30 @@
         @pl.when(s < out_r)
         def _():
             assemble_right(s)
-            for x in right(s):
-                x.start()
+            right(s)[0].start()
+
+            @pl.when(s >= quiet_out_r)
+            def _():
+                right(s)[1].start()
 
         @pl.when(has_left & (r >= 0) & (r < in_l))
         def _():
-            for x in left(r):
-                x.wait_recv()
+            left(r)[0].wait_recv()
             lc_o[r] = c_o[r]
-            lc_e[r] = c_e[r]
+
+            @pl.when(r >= quiet_in_l)
+            def _():
+                left(r)[1].wait_recv()
+                lc_e[r] = c_e[r]
 
         @pl.when(s < out_l)
         def _():
             assemble_left(s)
-            for x in left(s):
-                x.start()
+            left(s)[0].start()
+
+            @pl.when(s >= quiet_out_l)
+            def _():
+                left(s)[1].start()
 
         @pl.when(has_left & (p == dec_at))
         def _():
@@ -702,6 +721,11 @@
                 x.wait()
             for x in kv_far:
                 x.wait_recv()
+
+        @pl.when(s == 0)
+        def _():
+            for x in kv_own[1:]:
+                x.start()
 
         @pl.when(s < parts - 1)
         def _():
@@ -754,13 +778,21 @@
 
 
     def drain_right(p, carry):
-        for x in right(p):
-            x.wait_send()
+        right(p)[0].wait_send()
+
+        @pl.when(p >= quiet_out_r)
+        def _():
+            right(p)[1].wait_send()
+
         return carry
 
     def drain_left(p, carry):
-        for x in left(p):
-            x.wait_send()
+        left(p)[0].wait_send()
+
+        @pl.when(p >= quiet_out_l)
+        def _():
+            left(p)[1].wait_send()
+
         return carry
 
     for x in kv_far:
@@ -801,7 +833,7 @@
     heads = heads_all // sub_count
     width = query_width // sub_count
     parts = heads * group_size * rows // LANES
-    lengths, work, ready = stream_lengths(n, seq_dev, slots, parts)
+    lengths, work, ready, quiet = stream_lengths(n, seq_dev, slots, parts)
     count = max(lengths)
     bf, f32 = jnp.bfloat16, jnp.float32
     dec = heads * group_size * (seqs - slots)
@@ -840,7 +872,7 @@
     scratch += [dma((count,))] * 8 + [dma((6,))] * 2
     operands = (page_table, cached_len, is_prefill, queries, new_kv, kv_pages)
     return pl.pallas_call(
-        functools.partial(fused_kernel, n, lengths, work, ready, heads, group_size, rows, seq_dev, pages_dev),
+        functools.partial(fused_kernel, n, lengths, work, ready, quiet, heads, group_size, rows, seq_dev, pages_dev),
         out_shape=jax.ShapeDtypeStruct(queries.shape, queries.dtype),
         in_specs=[pl.BlockSpec(memory_space=pltpu.HBM)] * 6,
         out_specs=pl.BlockSpec(memory_space=pltpu.VMEM),

time: 72 us -> 71.6 us (level)
  no operation moved by 1% of the time
where the time goes in v9:
time: 71.6 us; the launch traced here: 71.4 us
  Pallas kernels  70.1 us (98%)
  local copies, waits for them, and re-layouts  1.32 us (2%)
    pallas_call x1, Pallas kernels, fused_attention(): pl.pallas_call(functools.partial(fused_kernel, n, lengths, work, ready, q...  70.1 us

profile of v9, /device:TPU:0, one launch (start us, length us, event | category | flops | bytes accessed | tf_op | source)
XLA Modules:
  0.0 71.4 jit_solution(16453062601647706330)
XLA Ops:
  0.0 70.1 %paged_attention.1 = bf16[4,64,4096]{2,1,0:T(8,128)(2,1)S(1)} custom-call(s32[16,16]{1,0:T(8,128)} %table_hbm.1, s32[16]{0:T(128)} %cached_hbm.1, s32[16]{0:T(128)} %flags_hbm.1, bf16[4,64,4096]{2,1,0:T(8,128)(2,1)} %q_hbm.1, bf16[4,64,2,512]{3,2,1,0:T(2,128)(2,1)} %new_hbm.1, bf16[21,2,128,512]{3,2,1,0:T(8,128)(2,1)} %kv_hbm.1), custom_call_target="tpu_custom_call" | custom-call | tf_op jit(solution)/shard_map/paged_attention/pallas_call | solution.py:874
  70.1 1.3 %copy.8 = bf16[4,64,4096]{2,1,0:T(8,128)(2,1)} copy(bf16[4,64,4096]{2,1,0:T(8,128)(2,1)S(1)} %paged_attention.1) | data formatting | bytes 4194304
